TPU v7x, 256 devices: a whole 4x4x8 slice. The times are simulated.
256 devices in a mesh: lat: 32 (over y_hi, z, core), ch: 8 (over y_lo, x).
Axes of the slice: x: 4, y: 4 (y_hi: 2, y_lo: 2; y = y_hi * 2 + y_lo), z: 8, core: 2. Of those that a mesh axis runs over, the one named last changes fastest.
Arguments:
- tokens: bfloat16 [32, 64, 138240], P(None, 'lat', 'ch'), may hold values from -60 to 60
- norm_gain: float32 [768], P('ch'), may hold values from 0.25 to 1.75
- norm_shift: float32 [768], P('ch'), may hold values from -1.5 to 1.5
- first_weight: float32 [2, 8, 96, 96], P(None, 'ch'), may hold values from -0.625 to 0.625
- first_bias: float32 [2, 8, 96], P(None, 'ch'), may hold values from -1.5 to 1.5
- second_weight: float32 [2, 8, 96, 96], P(None, 'ch'), may hold values from -0.625 to 0.625
- second_bias: float32 [2, 8, 96], P(None, 'ch'), may hold values from -1.5 to 1.5
- upstream: bfloat16 [32, 64, 138240], P(None, 'lat', 'ch'), may hold values from -6 to 6
Outputs:
- result: bfloat16 [32, 64, 138240], P(None, 'lat', 'ch')
- grad_tokens: bfloat16 [32, 64, 138240], P(None, 'lat', 'ch')
- grad_first_weight: float32 [2, 8, 96, 96], P(None, 'ch')
- grad_first_bias: float32 [2, 8, 96], P(None, 'ch')
- grad_second_weight: float32 [2, 8, 96, 96], P(None, 'ch')
- grad_second_bias: float32 [2, 8, 96], P(None, 'ch')
- grad_norm_gain: float32 [768], P('ch')
- grad_norm_shift: float32 [768], P('ch')
All inputs are finite; a program needn't handle non-finite values.
Results may differ from a plain program's by a relative error of at most 0.0086.
Values may be sent and summed in bfloat16 or wider, within the bound.
A program may use at most 192 MiB of HBM per device.

v0:
```python
import math

import jax
import jax.numpy as jnp
from jax import lax
from jax.sharding import Mesh
from jax.sharding import PartitionSpec as P

EMBED = 768
LAT = ("lat_0", "lat_1", "lat_2")


layer_eps = 1e-05
shrink_level = 0.1
highest = lax.Precision.HIGHEST


def from_everyone(x, axis):
    peers = lax.axis_size(axis)
    return lax.all_to_all(jnp.broadcast_to(x[None], (peers, *x.shape)), axis, 0, 0, tiled=True)


def over_copies(x, axis):
    return from_everyone(x, axis).sum(axis=0)


def together(arrays, axis):
    line, at, finished = (jnp.concatenate([a.reshape(-1) for a in arrays]), 0, [])
    so_far = over_copies(line, axis)
    for a in arrays:
        finished.append(so_far[at : at + a.size].reshape(a.shape))
        at += a.size
    return tuple(finished)


def cut_along(x, dim, peers):
    dims = x.shape
    parts = x.reshape(*dims[:dim], peers, dims[dim] // peers, *dims[dim + 1 :])
    return jnp.moveaxis(parts, dim, 0)


def in_order(parts, dim):
    parts = jnp.moveaxis(parts, 0, dim)
    dims = parts.shape
    return parts.reshape(*dims[:dim], dims[dim] * dims[dim + 1], *dims[dim + 2 :])


def moved_by_axis(parts, axes, order):
    dims = [lax.axis_size(a) for a in axes]
    parts = parts.reshape(*dims, *parts.shape[1:])
    for k in order:
        parts = lax.all_to_all(parts, axes[k], split_axis=k, concat_axis=k, tiled=True)
    return parts.reshape(-1, *parts.shape[len(axes) :])


def exchange_by_chip(x, groups, order, split_dim, concat_dim):
    peers = lax.axis_size(groups[0]) * lax.axis_size(groups[1])
    parts = cut_along(x, split_dim, peers)
    return in_order(moved_by_axis(parts, groups, order), concat_dim)


def angle_table(length, columns):
    row_index = lax.broadcasted_iota(jnp.int32, (length, columns), 0)
    col_index = lax.broadcasted_iota(jnp.int32, (length, columns), 1)
    return 2.0 * math.pi / length * (row_index * col_index % length).astype(jnp.float32)


def longitude_tables(length):
    modes_count = length // 2 + 1
    angles = angle_table(length, modes_count)
    factor = 1.0 / math.sqrt(length)
    mode_index = lax.broadcasted_iota(jnp.int32, (1, modes_count), 1)
    doubled = jnp.where((mode_index == 0) | (mode_index * 2 == length), 1.0, 2.0)
    forward_cos = jnp.cos(angles) * factor
    forward_sin = -jnp.sin(angles) * factor
    return (
        forward_cos,
        forward_sin,
        jnp.transpose(forward_cos * doubled),
        jnp.transpose(forward_sin * doubled),
    )


def row_forward(field_in):
    tables = longitude_tables(field_in.shape[3])
    real_part = jnp.einsum("bhcw,wk->bhkc", field_in, tables[0], precision=highest)
    imag_part = jnp.einsum("bhcw,wk->bhkc", field_in, tables[1], precision=highest)
    return (real_part, imag_part)


def row_inverse(real_part, imag_part):
    length = 2 * (real_part.shape[2] - 1)
    tables = longitude_tables(length)
    return jnp.einsum("bhkc,kw->bhcw", real_part, tables[2], precision=highest) + jnp.einsum(
        "bhkc,kw->bhcw", imag_part, tables[3], precision=highest
    )


def latitude_mix(table, values):
    return jnp.einsum("mh,bhkc->bmkc", table, values, precision=highest)


def latitude_transform(real_part, imag_part, direction):
    height = real_part.shape[1]
    angles = angle_table(height, height)
    cosine = jnp.cos(angles) / math.sqrt(height)
    sine_part = direction * jnp.sin(angles) / math.sqrt(height)
    new_real = latitude_mix(cosine, real_part) - latitude_mix(sine_part, imag_part)
    new_imag = latitude_mix(cosine, imag_part) + latitude_mix(sine_part, real_part)
    return (new_real, new_imag)


def block_mix(values, matrix):
    return jnp.einsum("bhknc,ncd->bhknd", values, matrix, precision=highest)


def smooth_gelu(values):
    return (
        0.5
        * values
        * (
            1.0
            + jnp.tanh(math.sqrt(2.0 / math.pi) * (values + 0.044715 * values * values * values))
        )
    )


def spectral_mlp(real_part, imag_part, params):
    first_weight, first_bias, second_weight, second_bias = params
    dims_shape = real_part.shape
    groups = first_weight.shape[1]
    block_width = first_weight.shape[2]
    real_part = real_part.reshape(dims_shape[:-1] + (groups, block_width))
    imag_part = imag_part.reshape(dims_shape[:-1] + (groups, block_width))
    hidden_real = smooth_gelu(
        block_mix(real_part, first_weight[0])
        - block_mix(imag_part, first_weight[1])
        + first_bias[0]
    )
    hidden_imag = smooth_gelu(
        block_mix(imag_part, first_weight[0])
        + block_mix(real_part, first_weight[1])
        + first_bias[1]
    )
    mixed_real = (
        block_mix(hidden_real, second_weight[0])
        - block_mix(hidden_imag, second_weight[1])
        + second_bias[0]
    )
    mixed_imag = (
        block_mix(hidden_imag, second_weight[0])
        + block_mix(hidden_real, second_weight[1])
        + second_bias[1]
    )
    mixed_real = mixed_real - shrink_level * jnp.tanh(mixed_real / shrink_level)
    mixed_imag = mixed_imag - shrink_level * jnp.tanh(mixed_imag / shrink_level)
    return (mixed_real.reshape(dims_shape), mixed_imag.reshape(dims_shape))


def column_spectral(spectra, params):
    real_part, imag_part = latitude_transform(spectra[0], spectra[1], -1.0)
    real_part, imag_part = spectral_mlp(real_part, imag_part, params)
    return latitude_transform(real_part, imag_part, 1.0)


def column_filter(field_in, params):
    mixed_spec = column_spectral(row_forward(field_in), params)
    return row_inverse(mixed_spec[0], mixed_spec[1])


def channel_sums(first_term, second_term):
    return together((jnp.sum(first_term, axis=-2), jnp.sum(second_term, axis=-2)), "ch")


def fields_columns(field_in):
    return lax.all_to_all(field_in, LAT, split_axis=0, concat_axis=1, tiled=True)


def fields_rows(field_in):
    return exchange_by_chip(field_in, (("lat_0", "lat_1"), "lat_2"), (1, 0), 1, 0)


def body(
    tokens, norm_gain, norm_shift, first_weight, first_bias, second_weight, second_bias, upstream
):
    params = (first_weight, first_bias, second_weight, second_bias)
    samples, rows_here, merged = tokens.shape
    channels = norm_gain.shape[0]
    width = merged // channels
    field_shape = (samples, rows_here, channels, width)
    gain_column = norm_gain[:, None]
    shift_column = norm_shift[:, None]
    as_float = tokens.reshape(field_shape).astype(jnp.float32)
    totals, squares = channel_sums(as_float, as_float * as_float)
    center = totals[..., None, :] / EMBED
    variance = squares[..., None, :] / EMBED - center * center
    inv_scale = lax.rsqrt(variance + layer_eps)
    standard = (as_float - center) * inv_scale
    normed = lax.optimization_barrier((standard * gain_column + shift_column).astype(jnp.bfloat16))
    normed_float = normed.astype(jnp.float32)
    grad_out = upstream.reshape(field_shape).astype(jnp.float32)
    normed_columns = fields_columns(normed.reshape(samples, rows_here, merged))
    column_shape = normed_columns.shape[:2] + (channels, width)
    filtered_columns, column_pull = jax.vjp(
        column_filter, normed_columns.reshape(column_shape).astype(jnp.float32), params
    )
    filtered = fields_rows(
        filtered_columns.astype(jnp.bfloat16).reshape(column_shape[0], column_shape[1], merged)
    )
    filtered = filtered.reshape(field_shape)
    upstream_columns = fields_columns(upstream)
    field_grad, param_grads = column_pull(
        upstream_columns.reshape(column_shape).astype(jnp.float32)
    )
    spectral_grad = fields_rows(
        field_grad.astype(jnp.bfloat16).reshape(column_shape[0], column_shape[1], merged)
    )
    spectral_grad = spectral_grad.reshape(field_shape)
    result = (as_float + normed_float + filtered.astype(jnp.float32)).astype(jnp.bfloat16)
    normed_grad = grad_out + spectral_grad.astype(jnp.float32)
    gain_part = jnp.sum(normed_grad * standard, axis=(0, 1, 3))
    shift_part = jnp.sum(normed_grad, axis=(0, 1, 3))
    standard_grad = normed_grad * gain_column
    grad_mean, grad_cross = channel_sums(standard_grad, standard_grad * standard)
    grad_tokens = (
        grad_out
        + inv_scale
        * (
            standard_grad
            - grad_mean[..., None, :] / EMBED
            - standard * (grad_cross[..., None, :] / EMBED)
        )
    ).astype(jnp.bfloat16)
    summed = together(
        (param_grads[0], param_grads[1], param_grads[2], param_grads[3], gain_part, shift_part), LAT
    )
    return (
        result.reshape(samples, rows_here, merged),
        grad_tokens.reshape(samples, rows_here, merged),
        summed[0],
        summed[1],
        summed[2],
        summed[3],
        summed[4],
        summed[5],
    )


def solution(mesh):
    finer = Mesh(mesh.devices.reshape(2, 8, 2, mesh.shape["ch"]), ("lat_0", "lat_1", "lat_2", "ch"))
    return jax.shard_map(
        body,
        mesh=finer,
        in_specs=(
            P(None, LAT, "ch"),
            P("ch"),
            P("ch"),
            P(None, "ch", None, None),
            P(None, "ch", None),
            P(None, "ch", None, None),
            P(None, "ch", None),
            P(None, LAT, "ch"),
        ),
        out_specs=(
            P(None, LAT, "ch"),
            P(None, LAT, "ch"),
            P(None, "ch", None, None),
            P(None, "ch", None),
            P(None, "ch", None, None),
            P(None, "ch", None),
            P("ch"),
            P("ch"),
        ),
        check_vma=False,
    )
```

profile of v0, /device:TPU:1, one launch (start us, length us, event | category | flops | bytes accessed | tf_op | source)
XLA Modules:
  0.0 777.1 jit_solution(4066731010136854337)
XLA Ops:
  4.7 11.4 %reshape.607 = f32[32,2,96,180]{3,2,0,1:T(8,128)} reshape(f32[32,2,17280]{2,0,1:T(8,128)} %copy_convert_fusion.1) | data formatting | bytes 8847360 | tf_op jit(solution)/shard_map/convert_element_type | solution.py:193
  21.8 17.3 %all_to_all.56 = f32[8,1,23040]{2,1,0:T(1,128)S(1)} all-to-all(f32[8,1,23040]{2,1,0:T(1,128)S(1)} %broadcast_in_dim.62), channel_id=1, replica_groups=mesh['lat_0'=2,'lat_1'=8,'lat_2'=2,'ch'=8] {'ch'}, dimensions={0} | all-to-all | bytes 1474560 | tf_op jit(solution)/shard_map/all_to_all | solution.py:20
  39.1 12.8 %all-to-all-start.4 = ((bf16[32,2,17280]{2,1,0:T(2,128)(2,1)}), bf16[32,2,17280]{2,1,0:T(2,128)(2,1)}, u32[]{:S(2)}, u32[]{:S(2)}) async-start(bf16[32,2,17280]{2,1,0:T(2,128)(2,1)} %param.15), calls=%async_computation.4 | async-start | bytes 4423680 | tf_op jit(solution)/shard_map/all_to_all | solution.py:176
  66.8 38.4 %all-to-all-done.4 = bf16[32,2,17280]{2,1,0:T(2,128)(2,1)} async-done(((bf16[32,2,17280]{2,1,0:T(2,128)(2,1)}), bf16[32,2,17280]{2,1,0:T(2,128)(2,1)}, u32[]{:S(2)}, u32[]{:S(2)}) %all-to-all-start.4) | async-done | bytes 2211872 | tf_op jit(solution)/shard_map/all_to_all | solution.py:176
  111.0 12.0 %reshape.578 = bf16[64,96,180]{2,1,0:T(8,128)(2,1)S(1)} reshape(bf16[32,2,17280]{2,1,0:T(2,128)(2,1)} %all-to-all-done.4) | data formatting | bytes 4423680 | tf_op jit(solution)/shard_map/reshape.98
  133.3 18.8 %fusion.113 = f32[91,96,64]{1,2,0:T(8,128)} fusion(f32[91,96,64]{1,0,2:T(8,128)S(1)} %convolution_bitcast_fusion), kind=kOutput, calls=%fused_computation.159 | convolution fusion | flops 429453312 | bytes 4472832 | tf_op jit(solution)/shard_map/transpose(jvp(mh,bhkc->bmkc))/dot_general | solution.py:100
  164.3 11.7 %reshape.562 = bf16[64,96,180]{2,1,0:T(8,128)(2,1)S(1)} reshape(bf16[32,2,17280]{2,1,0:T(2,128)(2,1)} %all-to-all-done.1) | data formatting | bytes 4423680 | tf_op jit(solution)/shard_map/reshape.3
  282.6 9.9 %add_convert_fusion.2 = bf16[64,96,180]{1,2,0:T(8,128)(2,1)} fusion(f32[64,96,180]{1,2,0:T(8,128)S(1)} %fusion.11, f32[64,91,96]{2,0,1:T(8,128)S(1)} %subtract_bitcast_fusion, f32[91]{0:T(128)S(1)} %fusion.342), kind=kOutput, calls=%fused_computation.9 | convolution fusion | flops 1210040320 | bytes 8872300 | tf_op jit(solution)/shard_map/jvp(bhkc,kw->bhcw)/dot_general | solution.py:94
  297.3 9.8 %reshape_transpose_reshape_reshape.6 = bf16[16,2,1,2,17280]{4,3,1,0,2:T(2,128)(2,1)} reshape(bf16[64,96,180]{2,1,0:T(8,128)(2,1)} %copy.538) | data formatting | bytes 4423680 | tf_op jit(solution)/shard_map/reshape;transpose;reshape;reshape | solution.py:50
  349.9 7.1 fusion.3
  367.0 12.0 %add_convert_fusion.1 = bf16[64,96,180]{1,2,0:T(8,128)(2,1)} fusion(f32[64,96,180]{1,2,0:T(8,128)S(1)} %fusion.3, f32[91,64,96]{2,1,0:T(8,128)S(1)} %add_bitcast_fusion.2), kind=kOutput, calls=%fused_computation.8 | convolution fusion | flops 1210056704 | bytes 8871936 | tf_op jit(solution)/shard_map/transpose(jvp(bhcw,wk->bhkc))/dot_general | solution.py:87
  383.7 9.8 %reshape_transpose_reshape_reshape.7 = bf16[16,2,1,2,17280]{4,3,1,0,2:T(2,128)(2,1)} reshape(bf16[64,96,180]{2,1,0:T(8,128)(2,1)} %copy.567) | data formatting | bytes 4423680 | tf_op jit(solution)/shard_map/reshape;transpose;reshape;reshape | solution.py:50
  416.3 48.0 %all-to-all-done.3 = bf16[16,2,1,2,17280]{4,3,1,2,0:T(2,128)(2,1)} async-done(((bf16[16,2,1,2,17280]{4,3,1,2,0:T(2,128)(2,1)}), bf16[16,2,1,2,17280]{4,3,1,2,0:T(2,128)(2,1)}, u32[]{:S(2)}, u32[]{:S(2)}) %all-to-all-start.3) | async-done | bytes 2211872 | tf_op jit(solution)/shard_map/all_to_all | solution.py:52
  464.3 8.6 %all-to-all-start.6 = ((bf16[16,2,1,2,17280]{4,3,1,2,0:T(2,128)(2,1)}), bf16[16,2,1,2,17280]{4,3,1,2,0:T(2,128)(2,1)}, u32[]{:S(2)}, u32[]{:S(2)}) async-start(bf16[16,2,1,2,17280]{4,3,1,2,0:T(2,128)(2,1)} %copy.569), calls=%async_computation.6 | async-start | bytes 4423680 | tf_op jit(solution)/shard_map/all_to_all | solution.py:52
  477.1 11.4 %reshape.610 = f32[32,2,96,180]{3,2,0,1:T(8,128)} reshape(f32[32,2,17280]{2,0,1:T(8,128)} %copy_convert_fusion) | data formatting | bytes 8847360 | tf_op jit(solution)/shard_map/convert_element_type | solution.py:201
  501.5 7.2 mul.417
  508.8 8.4 %fusion.183 = f32[1,1,96,96]{2,3,1,0:T(8,128)S(1)} fusion(f32[1,64,91,1,96]{4,1,2,3,0:T(8,128)} %copy-done.22, f32[1,64,91,1,96]{4,1,2,3,0:T(8,128)} %copy-done.10), kind=kOutput, calls=%fused_computation.190 | convolution fusion | flops 648560640 | bytes 4509696 | tf_op jit(solution)/shard_map/transpose(jvp(bhknc,ncd->bhknd))/dot_general | solution.py:114
  534.7 8.1 %fusion.177 = f32[1,1,96,96]{2,3,1,0:T(8,128)S(1)} fusion(f32[91,96,64]{1,2,0:T(8,128)} %copy-done, f32[1,64,91,1,96]{4,1,2,3,0:T(8,128)} %get-tuple-element.89), kind=kOutput, calls=%fused_computation.188 | convolution fusion | flops 644087808 | bytes 4509696 | tf_op jit(solution)/shard_map/transpose(jvp(bhknc,ncd->bhknd))/dot_general | solution.py:114
  547.9 12.2 %reshape.608 = f32[32,2,96,180]{3,2,1,0:T(8,128)} reshape(bf16[16,2,1,2,17280]{4,3,1,2,0:T(2,128)(2,1)} %all-to-all-done.3) | data formatting | bytes 6635520 | tf_op jit(solution)/shard_map/convert_element_type | solution.py:219
  560.1 12.2 %reshape.611 = f32[32,2,96,180]{3,2,1,0:T(8,128)} reshape(bf16[16,2,1,2,17280]{4,3,1,2,0:T(2,128)(2,1)} %all-to-all-done.6) | data formatting | bytes 6635520 | tf_op jit(solution)/shard_map/convert_element_type | solution.py:220
  572.3 13.0 %fusion.203 = (f32[32,2,180]{2,0,1:T(8,128)S(1)}, f32[32,2,180]{2,0,1:T(8,128)S(1)}, bf16[32,2,96,180]{3,2,0,1:T(8,128)(2,1)}) fusion(f32[96]{0:T(128)S(1)} %copy-done.26, f32[32,2,96,180]{3,2,0,1:T(8,128)} %reshape.610, f32[32,2,96,180]{3,2,1,0:T(8,128)} %reshape.611, f32[32,2,180]{2,0,1:T(8,128)S(1)} %copy.504, f32[32,2,96,180]{3,2,0,1:T(8,128)} %reshape.607, ...), kind=kLoop, calls=%fused_computation.194 | loop fusion | flops 12142080 | bytes 22303104 | tf_op jit(solution)/shard_map/reduce_sum | solution.py:172
  631.3 11.0 %fusion.162 = (f32[17280]{0:T(1024)S(1)}, f32[17280]{0:T(1024)S(1)}, bf16[32,2,17280]{2,0,1:T(8,128)(2,1)}) fusion(f32[32,2,17280]{2,1,0:T(2,128)} %bitcast.530, bf16[32,2,17280]{2,1,0:T(2,128)(2,1)} %param.15, f32[32,2,17280]{2,0,1:T(8,128)} %mul.417, f32[32,2,17280]{2,0,1:T(8,128)} %sub.117, bf16[32,2,17280]{2,1,0:T(2,128)(2,1)S(1)} %copy-done.18, ...), kind=kLoop, calls=%fused_computation.177 | loop fusion | flops 16554240 | bytes 28961280 | tf_op jit(solution)/shard_map/reduce_sum | solution.py:222
  647.6 11.5 %all-to-all-start.8 = ((f32[32,1,37440]{2,1,0:T(1,128)}), f32[32,1,37440]{2,1,0:T(1,128)}, u32[]{:S(2)}, u32[]{:S(2)}) async-start(f32[32,1,37440]{2,1,0:T(1,128)} %broadcast_in_dim.78), calls=%async_computation.8 | async-start | bytes 9601024 | tf_op jit(solution)/shard_map/all_to_all | solution.py:20
  671.8 96.2 %all-to-all-done.8 = f32[32,1,37440]{2,1,0:T(1,128)} async-done(((f32[32,1,37440]{2,1,0:T(1,128)}), f32[32,1,37440]{2,1,0:T(1,128)}, u32[]{:S(2)}, u32[]{:S(2)}) %all-to-all-start.8) | async-done | bytes 4792352 | tf_op jit(solution)/shard_map/all_to_all | solution.py:20
  (195 shorter events, 356.0 us)
Async XLA Ops:
  39.1 13.8 %copy-start.26 = (f32[96]{0:T(128)S(1)}, f32[96]{0:T(128)}, u32[]{:S(2)}) copy-start(f32[96]{0:T(128)} %param.9) | copy-start | bytes 1156
  39.1 13.8 %copy-start.30 = (f32[96]{0:T(128)S(1)}, f32[96]{0:T(128)}, u32[]{:S(2)}) copy-start(f32[96]{0:T(128)} %param.10) | copy-start | bytes 1156
  39.1 66.1 %all-to-all-start.4 = ((bf16[32,2,17280]{2,1,0:T(2,128)(2,1)}), bf16[32,2,17280]{2,1,0:T(2,128)(2,1)}, u32[]{:S(2)}, u32[]{:S(2)}) async-start(bf16[32,2,17280]{2,1,0:T(2,128)(2,1)} %param.15), calls=%async_computation.4 | async-start | bytes 4423680 | tf_op jit(solution)/shard_map/all_to_all | solution.py:176
  57.2 9.5 %copy-start.7 = (bf16[32,2,96,180]{3,2,0,1:T(8,128)(2,1)}, bf16[32,2,96,180]{3,2,0,1:T(8,128)(2,1)S(1)}, u32[]{:S(2)}) copy-start(bf16[32,2,96,180]{3,2,0,1:T(8,128)(2,1)S(1)} %add_convert_fusion) | copy-start | bytes 6635524
  66.8 44.2 %copy-start.28 = (f32[2,1,96]{2,1,0:T(1,128)S(1)}, f32[2,1,96]{2,1,0:T(1,128)}, u32[]{:S(2)}) copy-start(f32[2,1,96]{2,1,0:T(1,128)} %param.12) | copy-start | bytes 2308
  66.8 44.2 %copy-start.29 = (f32[2,1,96]{2,1,0:T(1,128)S(1)}, f32[2,1,96]{2,1,0:T(1,128)}, u32[]{:S(2)}) copy-start(f32[2,1,96]{2,1,0:T(1,128)} %param.14) | copy-start | bytes 2308
  105.2 59.1 %all-to-all-start.1 = ((bf16[32,2,17280]{2,1,0:T(2,128)(2,1)}), bf16[32,2,17280]{2,1,0:T(2,128)(2,1)}, u32[]{:S(2)}, u32[]{:S(2)}) async-start(bf16[32,2,17280]{2,1,0:T(2,128)(2,1)} %copy.505), calls=%async_computation.1 | async-start | bytes 4423680 | tf_op jit(solution)/shard_map/all_to_all | solution.py:176
  199.1 17.3 %copy-start = (f32[91,96,64]{1,2,0:T(8,128)}, f32[91,96,64]{1,2,0:T(8,128)S(1)}, u32[]{:S(2)}) copy-start(f32[91,96,64]{1,2,0:T(8,128)S(1)} %fusion.132) | copy-start | bytes 6709252
  209.5 48.7 %copy-start.20 = (f32[1,64,91,1,96]{4,1,2,3,0:T(8,128)}, f32[1,64,91,1,96]{4,1,2,3,0:T(8,128)S(1)}, u32[]{:S(2)}) copy-start(f32[1,64,91,1,96]{4,1,2,3,0:T(8,128)S(1)} %fusion.31) | copy-start | bytes 6709252
  221.8 31.5 %copy-start.10 = (f32[1,64,91,1,96]{4,1,2,3,0:T(8,128)}, f32[1,64,91,1,96]{4,1,2,3,0:T(8,128)S(1)}, u32[]{:S(2)}) copy-start(f32[1,64,91,1,96]{4,1,2,3,0:T(8,128)S(1)} %fusion.32) | copy-start | bytes 6709252
  240.3 7.3 copy-start.16
  258.2 14.7 %copy-start.3 = (f32[1,64,91,1,96]{4,1,2,3,0:T(8,128)}, f32[1,64,91,1,96]{4,1,2,3,0:T(8,128)S(1)}, u32[]{:S(2)}) copy-start(f32[1,64,91,1,96]{4,1,2,3,0:T(8,128)S(1)} %fusion.21) | copy-start | bytes 6709252
  311.6 86.4 %all-to-all-start.2 = ((bf16[16,2,1,2,17280]{4,3,0,2,1:T(2,128)(2,1)}), bf16[16,2,1,2,17280]{4,3,0,2,1:T(2,128)(2,1)}, u32[]{:S(2)}, u32[]{:S(2)}) async-start(bf16[16,2,1,2,17280]{4,3,0,2,1:T(2,128)(2,1)} %copy.539), calls=%async_computation.2 | async-start | bytes 4423680 | tf_op jit(solution)/shard_map/all_to_all | solution.py:52
  398.0 9.4 %all-to-all-start.5 = ((bf16[16,2,1,2,17280]{4,3,0,2,1:T(2,128)(2,1)}), bf16[16,2,1,2,17280]{4,3,0,2,1:T(2,128)(2,1)}, u32[]{:S(2)}, u32[]{:S(2)}) async-start(bf16[16,2,1,2,17280]{4,3,0,2,1:T(2,128)(2,1)} %copy.568), calls=%async_computation.5 | async-start | bytes 4423680 | tf_op jit(solution)/shard_map/all_to_all | solution.py:52
  407.4 57.0 %all-to-all-start.3 = ((bf16[16,2,1,2,17280]{4,3,1,2,0:T(2,128)(2,1)}), bf16[16,2,1,2,17280]{4,3,1,2,0:T(2,128)(2,1)}, u32[]{:S(2)}, u32[]{:S(2)}) async-start(bf16[16,2,1,2,17280]{4,3,1,2,0:T(2,128)(2,1)} %copy.540), calls=%async_computation.3 | async-start | bytes 4423680 | tf_op jit(solution)/shard_map/all_to_all | solution.py:52
  464.3 95.8 %all-to-all-start.6 = ((bf16[16,2,1,2,17280]{4,3,1,2,0:T(2,128)(2,1)}), bf16[16,2,1,2,17280]{4,3,1,2,0:T(2,128)(2,1)}, u32[]{:S(2)}, u32[]{:S(2)}) async-start(bf16[16,2,1,2,17280]{4,3,1,2,0:T(2,128)(2,1)} %copy.569), calls=%async_computation.6 | async-start | bytes 4423680 | tf_op jit(solution)/shard_map/all_to_all | solution.py:52
  508.8 8.4 %copy-start.21 = (f32[1,64,91,1,96]{4,1,2,3,0:T(8,128)S(1)}, f32[1,64,91,1,96]{4,1,2,3,0:T(8,128)}, u32[]{:S(2)}) copy-start(f32[1,64,91,1,96]{4,1,2,3,0:T(8,128)} %copy-done.20) | copy-start | bytes 6709252
  508.8 8.4 %copy-start.23 = (f32[1,64,91,1,96]{4,1,2,3,0:T(8,128)S(1)}, f32[1,64,91,1,96]{4,1,2,3,0:T(8,128)}, u32[]{:S(2)}) copy-start(f32[1,64,91,1,96]{4,1,2,3,0:T(8,128)} %copy-done.22) | copy-start | bytes 6709252
  534.7 8.2 %copy-start.1 = (f32[91,96,64]{1,2,0:T(8,128)S(1)}, f32[91,96,64]{1,2,0:T(8,128)}, u32[]{:S(2)}) copy-start(f32[91,96,64]{1,2,0:T(8,128)} %copy-done) | copy-start | bytes 6709252
  534.7 8.2 %copy-start.5 = (f32[1,64,91,1,96]{4,1,2,3,0:T(8,128)S(1)}, f32[1,64,91,1,96]{4,1,2,3,0:T(8,128)}, u32[]{:S(2)}) copy-start(f32[1,64,91,1,96]{4,1,2,3,0:T(8,128)} %copy-done.3) | copy-start | bytes 6709252
  587.0 21.9 %all-to-all-start.7 = ((f32[8,1,23040]{2,1,0:T(1,128)}), f32[8,1,23040]{2,1,0:T(1,128)}, u32[]{:S(2)}, u32[]{:S(2)}) async-start(f32[8,1,23040]{2,1,0:T(1,128)} %broadcast_in_dim.65), calls=%async_computation.7 | async-start | bytes 1474560 | tf_op jit(solution)/shard_map/all_to_all | solution.py:20
  624.3 7.0 copy-start.18
  647.6 11.5 %copy-start.14 = (bf16[32,2,96,180]{3,2,0,1:T(8,128)(2,1)S(1)}, bf16[32,2,96,180]{3,2,0,1:T(8,128)(2,1)}, u32[]{:S(2)}) copy-start(bf16[32,2,96,180]{3,2,0,1:T(8,128)(2,1)} %get-tuple-element.71) | copy-start | bytes 6635524
  647.6 120.5 %all-to-all-start.8 = ((f32[32,1,37440]{2,1,0:T(1,128)}), f32[32,1,37440]{2,1,0:T(1,128)}, u32[]{:S(2)}, u32[]{:S(2)}) async-start(f32[32,1,37440]{2,1,0:T(1,128)} %broadcast_in_dim.78), calls=%async_computation.8 | async-start | bytes 9601024 | tf_op jit(solution)/shard_map/all_to_all | solution.py:20
  (16 other events, 73.2 us)
where the time goes:
time: 788 us; the launch traced here: 777 us
  matrix products  257 us (33%)
  local copies, waits for them, and re-layouts  195 us (25%)
  waiting for transfers between devices  187 us (24%)
  other arithmetic  59.4 us (8%)
  starting transfers between devices  58.7 us (7%)
  blocking collectives  17.3 us (2%)
    dot_general x24, matrix products, block_mix(): return jnp.einsum('bhknc,ncd->bhknd', values, matrix, precision=highest)  114 us
    all_to_all x2, waiting for transfers between devices, from_everyone(): lax.all_to_all(jnp.broadcast_to(x[None], (peers, *x.shape)), axis, 0, 0,...  96.2 us
    dot_general x16, matrix products, latitude_mix(): return jnp.einsum('mh,bhkc->bmkc', table, values, precision=highest)  91 us
    all_to_all x4, waiting for transfers between devices, moved_by_axis(): lax.all_to_all(parts, axes[k], split_axis=k, concat_axis=k, tiled=True)  48 us
    all_to_all x2, waiting for transfers between devices, fields_columns(): lax.all_to_all(field_in, LAT, split_axis=0, concat_axis=1, tiled=True)  42.8 us
    another operation x4, local copies, waits for them, and re-layouts, moved_by_axis(): parts = parts.reshape(*dims, *parts.shape[1:])  28.6 us
    all_to_all x4, starting transfers between devices, moved_by_axis(): lax.all_to_all(parts, axes[k], split_axis=k, concat_axis=k, tiled=True)  24.3 us
    another operation x2, local copies, waits for them, and re-layouts  23.7 us
  transfers between devices with their start and end apart: 8, of which 4 were waited for; matrix products, arithmetic and copies ran while one was open for 34% of the time, Pallas kernels for 0%

commit v1 on v0

v1 whole, which is shorter than its diff:
```python
import functools
import math

import jax
import jax.numpy as jnp
import numpy as np
from jax import lax
from jax.experimental import pallas as pl
from jax.experimental.pallas import tpu as pltpu
from jax.sharding import Mesh
from jax.sharding import PartitionSpec as P

LAT_ROWS = 64
LON = 180
MODES = 91
CH = 96
GROUP = 32
GROUPS = CH // GROUP
SPAN = GROUP * LON
PITCH = 40
EMBED = 768
layer_eps = 1e-05
shrink = 0.1
f32 = jnp.float32
bf16 = jnp.bfloat16


def split_table(table):
    high = table.astype(np.float32).astype(bf16)
    low = (table - high.astype(np.float64)).astype(np.float32).astype(bf16)
    return high, low


@functools.cache
def tables():
    m = np.arange(33)[:, None]
    h = np.arange(LAT_ROWS)[None, :]
    ang = 2.0 * np.pi * ((m * h) % LAT_ROWS) / LAT_ROWS
    lat = np.concatenate([np.cos(ang), np.sin(ang)[1:32]], axis=0) / math.sqrt(LAT_ROWS)
    w = np.arange(LON)[:, None]
    k = np.arange(MODES)[None, :]
    ang = 2.0 * np.pi * ((w * k) % LON) / LON
    lon = np.zeros((256, 256))
    lon[:LON, :MODES] = np.cos(ang) / math.sqrt(LON)
    lon[:LON, 128 : 128 + MODES] = np.sin(ang) / math.sqrt(LON)
    lon[:LON, 128 + MODES - 1] = 0.0
    lon[:LON, 128] = 0.0
    double = np.zeros((256,))
    double[:MODES] = 2.0
    double[128 : 128 + MODES] = 2.0
    double[[0, MODES - 1, 128, 128 + MODES - 1]] = 1.0
    return lat, lon, lon * double[None, :]


def split(x):
    high = x.astype(bf16)
    return high, (x - high.astype(f32)).astype(bf16)


def dot(a, b):
    return jnp.dot(a, b, preferred_element_type=f32)


def dot_nt(a, b):
    return lax.dot_general(a, b, (((1,), (1,)), ((), ())), preferred_element_type=f32)


def to_spectrum_kernel(x_ref, lat_ref, lonh_ref, lonl_ref, re_ref, im_ref, zs, ya, yb):
    @pl.when(pl.program_id(0) == 0)
    def _():
        ya[...] = jnp.zeros_like(ya)
        yb[...] = jnp.zeros_like(yb)

    x = x_ref[...].reshape(LAT_ROWS, SPAN)
    both = dot(lat_ref[...], x)
    zs[...] = both[:LAT_ROWS] + both[LAT_ROWS:]
    for c in range(GROUP):
        v = zs[:, c * LON : (c + 1) * LON]
        ya[pl.ds(c, LAT_ROWS, stride=PITCH), :] = v[:, :128]
        yb[pl.ds(c, LAT_ROWS, stride=PITCH), 0 : LON - 128] = v[:, 128:]
    rows = jnp.concatenate([ya[...], yb[...]], axis=1)
    rows = rows.reshape(LAT_ROWS, PITCH, 256)[:, :GROUP].reshape(LAT_ROWS * GROUP, 256)
    high, low = split(rows)
    p = dot(high, lonh_ref[...]) + dot(low, lonh_ref[...]) + dot(high, lonl_ref[...])
    p = p.reshape(LAT_ROWS, GROUP, 256)
    cc, cs = p[:, :, :128], p[:, :, 128:]
    re_ref[0:1] = cc[0:1]
    im_ref[0:1] = -cs[0:1]
    re_ref[32:33] = cc[32:33]
    im_ref[32:33] = -cs[32:33]
    re_ref[1:32] = cc[1:32] - cs[33:64]
    re_ref[33:64] = cc[1:32] + cs[33:64]
    im_ref[1:32] = -cs[1:32] - cc[33:64]
    im_ref[33:64] = cc[33:64] - cs[1:32]


def to_spectrum(x, doubled):
    lat, lon, lon2 = tables()
    lat_h, lat_l = split_table(lat)
    lon_h, lon_l = split_table(lon2 if doubled else lon)
    lat_table = jnp.asarray(np.concatenate([lat_h, lat_l], axis=0))
    full = lambda *s: pl.BlockSpec(s, lambda i: (0,) * len(s))
    spec = pl.BlockSpec((LAT_ROWS, GROUP, 128), lambda i: (0, i, 0))
    shape = jax.ShapeDtypeStruct((LAT_ROWS, CH, 128), f32)
    return pl.pallas_call(
        to_spectrum_kernel,
        grid=(GROUPS,),
        in_specs=[pl.BlockSpec((32, 2, SPAN), lambda i: (0, 0, i)), full(128, 64), full(256, 256), full(256, 256)],
        out_specs=[spec, spec],
        out_shape=[shape, shape],
        scratch_shapes=[
            pltpu.VMEM((LAT_ROWS, SPAN), f32),
            pltpu.VMEM((LAT_ROWS * PITCH, 128), f32),
            pltpu.VMEM((LAT_ROWS * PITCH, 128), f32),
        ],
        cost_estimate=pl.CostEstimate(flops=8_000_000_000, bytes_accessed=9_000_000, transcendentals=0),
        compiler_params=pltpu.CompilerParams(vmem_limit_bytes=48 * 2**20),
        name="to_spectrum",
    )(x, lat_table, jnp.asarray(lon_h), jnp.asarray(lon_l))


def to_field_kernel(re_ref, im_ref, lath_ref, latl_ref, lonh_ref, lonl_ref, o_ref, zs, va, vb):
    gr, gi = re_ref[...], im_ref[...]
    left = jnp.concatenate([gr[0:1], gr[1:32] + gr[33:64], gr[32:33], gi[33:64] - gi[1:32]], axis=0)
    right = -jnp.concatenate([gi[0:1], gi[1:32] + gi[33:64], gi[32:33], gr[1:32] - gr[33:64]], axis=0)
    rows = jnp.concatenate([left, right], axis=2).reshape(LAT_ROWS * GROUP, 256).astype(bf16)
    v = dot(rows, lonh_ref[...]) + dot(rows, lonl_ref[...])
    v = v.reshape(LAT_ROWS, GROUP, 256)
    va[:, 0:GROUP, :] = v[:, :, :128]
    vb[:, 0:GROUP, :] = v[:, :, 128:]
    va2, vb2 = va.reshape(LAT_ROWS * PITCH, 128), vb.reshape(LAT_ROWS * PITCH, 128)
    for c in range(GROUP):
        zs[:, c * LON : c * LON + 128] = va2[pl.ds(c, LAT_ROWS, stride=PITCH), :]
        zs[:, c * LON + 128 : (c + 1) * LON] = vb2[pl.ds(c, LAT_ROWS, stride=PITCH), 0 : LON - 128]
    z = zs[...].astype(bf16)
    out = dot(lath_ref[...], z) + dot(latl_ref[...], z)
    o_ref[...] = out.astype(bf16).reshape(32, 2, SPAN)


def to_field(re, im, doubled):
    lat, lon, lon2 = tables()
    lat_h, lat_l = split_table(lat.T)
    lon_h, lon_l = split_table((lon2 if doubled else lon).T)
    full = lambda *s: pl.BlockSpec(s, lambda i: (0,) * len(s))
    spec = pl.BlockSpec((LAT_ROWS, GROUP, 128), lambda i: (0, i, 0))
    return pl.pallas_call(
        to_field_kernel,
        grid=(GROUPS,),
        in_specs=[spec, spec, full(64, 64), full(64, 64), full(256, 256), full(256, 256)],
        out_specs=pl.BlockSpec((32, 2, SPAN), lambda i: (0, 0, i)),
        out_shape=jax.ShapeDtypeStruct((32, 2, CH * LON), bf16),
        scratch_shapes=[
            pltpu.VMEM((LAT_ROWS, SPAN), f32),
            pltpu.VMEM((LAT_ROWS, PITCH, 128), f32),
            pltpu.VMEM((LAT_ROWS, PITCH, 128), f32),
        ],
        cost_estimate=pl.CostEstimate(flops=8_000_000_000, bytes_accessed=9_000_000, transcendentals=0),
        compiler_params=pltpu.CompilerParams(vmem_limit_bytes=48 * 2**20),
        name="to_field",
    )(re, im, jnp.asarray(lat_h), jnp.asarray(lat_l), jnp.asarray(lon_h), jnp.asarray(lon_l))


STEP = 8


def gather_modes(re, im):
    return jnp.concatenate([jnp.concatenate([re[j], im[j]], axis=0) for j in range(STEP)], axis=1)


def mlp_forward_kernel(
    re_ref, im_ref, w1_ref, b1_ref, w2_ref, b2_ref, ore_ref, oim_ref, s_ref, g_ref, h_ref, t_ref,
    w1h, w1l, w2h, w2l,
):
    @pl.when(pl.program_id(0) == 0)
    def _():
        w1h[...], w1l[...] = split(w1_ref[...])
        w2h[...], w2l[...] = split(w2_ref[...])

    x = gather_modes(re_ref[...], im_ref[...])
    xh, xl = split(x)
    pre = dot(w1h[...], xh) + dot(w1h[...], xl) + dot(w1l[...], xh) + b1_ref[...]
    a = math.sqrt(2.0 / math.pi)
    sq = pre * pre
    th = jnp.tanh(a * pre * (1.0 + 0.044715 * sq))
    half = 0.5 * (1.0 + th)
    hid = pre * half
    slope = half + 0.5 * pre * (1.0 - th * th) * (a * (1.0 + 3.0 * 0.044715 * sq))
    hh, hl = split(hid)
    pre2 = dot(w2h[...], hh) + dot(w2h[...], hl) + dot(w2l[...], hh) + b2_ref[...]
    t = jnp.tanh(pre2 * (1.0 / shrink))
    mixed = pre2 - shrink * t
    for j in range(STEP):
        ore_ref[j] = mixed[:CH, 128 * j : 128 * (j + 1)]
        oim_ref[j] = mixed[CH:, 128 * j : 128 * (j + 1)]
    s_ref[0] = xh
    g_ref[0] = slope.astype(bf16)
    h_ref[0] = hh
    t_ref[0] = (t * t).astype(bf16)


def mlp_forward(re, im, mats, bias):
    w1, w2 = mats
    b1, b2 = bias
    n = LAT_ROWS // STEP
    full = lambda *s: pl.BlockSpec(s, lambda i: (0,) * len(s))
    spec = pl.BlockSpec((STEP, CH, 128), lambda i: (i, 0, 0))
    shape = jax.ShapeDtypeStruct((LAT_ROWS, CH, 128), f32)
    sspec = pl.BlockSpec((1, 2 * CH, 128 * STEP), lambda i: (i, 0, 0))
    sshape = jax.ShapeDtypeStruct((n, 2 * CH, 128 * STEP), bf16)
    mat, vec = full(192, 192), full(192, 1)
    return pl.pallas_call(
        mlp_forward_kernel,
        grid=(n,),
        in_specs=[spec, spec, mat, vec, mat, vec],
        out_specs=[spec, spec] + [sspec] * 4,
        out_shape=[shape, shape] + [sshape] * 4,
        scratch_shapes=[pltpu.VMEM((192, 192), bf16)] * 4,
        cost_estimate=pl.CostEstimate(flops=8_000_000_000, bytes_accessed=24_000_000, transcendentals=0),
        compiler_params=pltpu.CompilerParams(vmem_limit_bytes=48 * 2**20),
        name="mlp_forward",
    )(re, im, w1, b1, w2, b2)


def mlp_backward_kernel(
    re_ref, im_ref, s_ref, g_ref, h_ref, t_ref, w1_ref, w2_ref,
    ore_ref, oim_ref, d1_ref, e1_ref, d2_ref, e2_ref, a1, a2, c1, c2,
):
    step = pl.program_id(0)

    @pl.when(step == 0)
    def _():
        for r in (a1, a2, c1, c2):
            r[...] = jnp.zeros_like(r)

    p2 = gather_modes(re_ref[...], im_ref[...]) * t_ref[0].astype(f32)
    p2h = p2.astype(bf16)
    p1 = dot(w2_ref[...], p2h) * g_ref[0].astype(f32)
    p1h = p1.astype(bf16)
    out = dot(w1_ref[...], p1h)
    for j in range(STEP):
        ore_ref[j] = out[:CH, 128 * j : 128 * (j + 1)]
        oim_ref[j] = out[CH:, 128 * j : 128 * (j + 1)]
    a2[...] += dot_nt(h_ref[0], p2h)
    a1[...] += dot_nt(s_ref[0], p1h)
    c2[...] += sum(p2[:, 128 * j : 128 * (j + 1)] for j in range(STEP))
    c1[...] += sum(p1[:, 128 * j : 128 * (j + 1)] for j in range(STEP))

    @pl.when(step == pl.num_programs(0) - 1)
    def _():
        for acc, out_ref in ((a1, d1_ref), (a2, d2_ref)):
            v = acc[...]
            out_ref[0] = v[:CH, :CH] + v[CH:, CH:]
            out_ref[1] = v[:CH, CH:] - v[CH:, :CH]
        for acc, out_ref in ((c1, e1_ref), (c2, e2_ref)):
            out_ref[...] = jnp.sum(acc[...], axis=1, keepdims=True)


def mlp_backward(re, im, stash, w1, w2):
    n = LAT_ROWS // STEP
    full = lambda *s: pl.BlockSpec(s, lambda i: (0,) * len(s))
    spec = pl.BlockSpec((STEP, CH, 128), lambda i: (i, 0, 0))
    shape = jax.ShapeDtypeStruct((LAT_ROWS, CH, 128), f32)
    sspec = pl.BlockSpec((1, 2 * CH, 128 * STEP), lambda i: (i, 0, 0))
    mat = full(192, 192)
    d, e = jax.ShapeDtypeStruct((2, CH, CH), f32), jax.ShapeDtypeStruct((192, 1), f32)
    return pl.pallas_call(
        mlp_backward_kernel,
        grid=(n,),
        in_specs=[spec, spec] + [sspec] * 4 + [mat, mat],
        out_specs=[spec, spec, full(2, CH, CH), full(192, 1), full(2, CH, CH), full(192, 1)],
        out_shape=[shape, shape, d, e, d, e],
        scratch_shapes=[pltpu.VMEM((192, 192), f32)] * 2 + [pltpu.VMEM((192, 128), f32)] * 2,
        cost_estimate=pl.CostEstimate(flops=8_000_000_000, bytes_accessed=24_000_000, transcendentals=0),
        compiler_params=pltpu.CompilerParams(vmem_limit_bytes=48 * 2**20),
        name="mlp_backward",
    )(re, im, *stash, w1, w2)


def big_matrix(weight):
    real, imag = weight[0, 0], weight[1, 0]
    return jnp.block([[real, imag], [-imag, real]])


def lane_parts(ref_or_value):
    return [slice(c * LON, (c + 1) * LON) for c in range(GROUP)]


def widen(dst, values):
    for part in lane_parts(dst):
        dst[:, part] = values


def narrow(src):
    total = None
    for part in lane_parts(src):
        v = src[:, part]
        total = v if total is None else total + v
    return total


def load_rows(ref):
    return ref[...].reshape(LAT_ROWS, SPAN).astype(f32)


def norm_sums_kernel(x_ref, o_ref, first, second):
    step = pl.program_id(0)

    @pl.when(step == 0)
    def _():
        first[...] = jnp.zeros_like(first)
        second[...] = jnp.zeros_like(second)

    x = load_rows(x_ref)
    first[...] += x
    second[...] += x * x

    @pl.when(step == pl.num_programs(0) - 1)
    def _():
        o_ref[:, 0:LON] = narrow(first)
        o_ref[:, LON : 2 * LON] = narrow(second)
        o_ref[:, 2 * LON :] = jnp.zeros((LAT_ROWS, 384 - 2 * LON), f32)


def prepare_norm(sums_ref, center, scale):
    sums = sums_ref[0]
    for p in range(1, sums_ref.shape[0]):
        sums = sums + sums_ref[p]
    mean = sums[:, 0:LON] * (1.0 / EMBED)
    variance = sums[:, LON : 2 * LON] * (1.0 / EMBED) - mean * mean
    widen(center, mean)
    widen(scale, lax.rsqrt(variance + layer_eps))


def normalize_kernel(x_ref, sums_ref, gain_ref, shift_ref, o_ref, center, scale):
    @pl.when(pl.program_id(0) == 0)
    def _():
        prepare_norm(sums_ref, center, scale)

    standard = (load_rows(x_ref) - center[...]) * scale[...]
    o_ref[...] = (standard * gain_ref[...] + shift_ref[...]).astype(bf16).reshape(32, 2, SPAN)


def result_kernel(x_ref, n_ref, f_ref, o_ref):
    total = x_ref[...].astype(f32) + n_ref[...].astype(f32) + f_ref[...].astype(f32)
    o_ref[...] = total.astype(bf16)


def result_rows_kernel(x_ref, n_ref, f_ref, o_ref):
    total = load_rows(x_ref) + load_rows(n_ref) + load_rows(f_ref)
    o_ref[...] = total.astype(bf16).reshape(32, 2, SPAN)


def grad_sums_kernel(
    x_ref, u_ref, s_ref, sums_ref, gain_ref, o_ref, part_ref, center, scale, first, second
):
    step = pl.program_id(0)

    @pl.when(step == 0)
    def _():
        prepare_norm(sums_ref, center, scale)
        first[...] = jnp.zeros_like(first)
        second[...] = jnp.zeros_like(second)

    standard = (load_rows(x_ref) - center[...]) * scale[...]
    grad = load_rows(u_ref) + load_rows(s_ref)
    cross = grad * standard
    gain = gain_ref[...]
    first[...] += grad * gain
    second[...] += cross * gain
    part_ref[0:1, :] = jnp.sum(cross, axis=0, keepdims=True)
    part_ref[1:2, :] = jnp.sum(grad, axis=0, keepdims=True)

    @pl.when(step == pl.num_programs(0) - 1)
    def _():
        o_ref[:, 0:LON] = narrow(first)
        o_ref[:, LON : 2 * LON] = narrow(second)
        o_ref[:, 2 * LON :] = jnp.zeros((LAT_ROWS, 384 - 2 * LON), f32)


def grad_tokens_kernel(
    x_ref, u_ref, s_ref, sums_ref, grads_ref, gain_ref, o_ref, center, scale, mean_grad, cross_grad
):
    @pl.when(pl.program_id(0) == 0)
    def _():
        prepare_norm(sums_ref, center, scale)
        sums = grads_ref[0]
        for p in range(1, grads_ref.shape[0]):
            sums = sums + grads_ref[p]
        widen(mean_grad, sums[:, 0:LON] * (1.0 / EMBED))
        widen(cross_grad, sums[:, LON : 2 * LON] * (1.0 / EMBED))

    inverse = scale[...]
    standard = (load_rows(x_ref) - center[...]) * inverse
    up = load_rows(u_ref)
    grad = (up + load_rows(s_ref)) * gain_ref[...]
    out = up + inverse * (grad - mean_grad[...] - standard * cross_grad[...])
    o_ref[...] = out.astype(bf16).reshape(32, 2, SPAN)


def row_call(kernel, name, ins, outs, scratch):
    field = pl.BlockSpec((32, 2, SPAN), lambda i: (0, 0, i))
    line = lambda rows: pl.BlockSpec((rows, SPAN), lambda i: (0, i))

    def spec(x):
        if x.shape == (32, 2, CH * LON):
            return field
        if x.ndim == 2 and x.shape[1] == CH * LON:
            return line(x.shape[0])
        return pl.BlockSpec(x.shape, lambda i: (0,) * x.ndim)

    many = len(outs) > 1
    return pl.pallas_call(
        kernel,
        grid=(GROUPS,),
        in_specs=[spec(x) for x in ins],
        out_specs=[spec(x) for x in outs] if many else spec(outs[0]),
        out_shape=list(outs) if many else outs[0],
        scratch_shapes=[pltpu.VMEM((LAT_ROWS, SPAN), f32)] * scratch,
        cost_estimate=pl.CostEstimate(flops=3_000_000_000, bytes_accessed=8_000_000, transcendentals=0),
        compiler_params=pltpu.CompilerParams(vmem_limit_bytes=48 * 2**20),
        name=name,
    )(*ins)


FIELD = jax.ShapeDtypeStruct((32, 2, CH * LON), bf16)
SUMS = jax.ShapeDtypeStruct((LAT_ROWS, 384), f32)


def exchange(x, axes):
    return lax.all_to_all(x, axes, 0, 0, tiled=True)


def from_everyone(x, axes):
    peers = lax.axis_size(axes)
    return exchange(jnp.broadcast_to(x[None], (peers, *x.shape)), axes)


def reduced(line, axes):
    peers = lax.axis_size(axes)
    size = -(-line.size // (peers * 128)) * 128
    line = jnp.pad(line, (0, peers * size - line.size))
    mine = exchange(line.reshape(peers, 1, size), axes).sum(axis=0)
    return lax.all_gather(mine, axes, axis=0, tiled=True).reshape(-1)


def body(
    tokens, norm_gain, norm_shift, first_weight, first_bias, second_weight, second_bias, upstream
):
    lat = ("lat",)
    wide = lambda v: jnp.broadcast_to(v[:, None], (CH, LON)).reshape(1, CH * LON)
    gain, shift = wide(norm_gain), wide(norm_shift)
    first, second = big_matrix(first_weight), big_matrix(second_weight)
    bias = (first_bias.reshape(2 * CH, 1), second_bias.reshape(2 * CH, 1))

    upstream_columns = exchange(upstream, lat)
    sums = from_everyone(row_call(norm_sums_kernel, "norm_sums", (tokens,), (SUMS,), 2), "ch")
    normed = row_call(normalize_kernel, "normalize", (tokens, sums, gain, shift), (FIELD,), 2)
    normed_columns = exchange(normed, lat)
    up_re, up_im = to_spectrum(upstream_columns, True)
    re, im = to_spectrum(normed_columns, False)
    re, im, *stash = mlp_forward(re, im, (first.T, second.T), bias)
    filtered = exchange(to_field(re, im, True), lat)
    re, im, d1, e1, d2, e2 = mlp_backward(
        up_re, up_im, stash, first.astype(bf16), second.astype(bf16)
    )
    spectral = exchange(to_field(re, im, False), lat)
    result = row_call(result_kernel, "result", (tokens, normed, filtered), (FIELD,), 0)
    line = reduced(jnp.concatenate([a.reshape(-1) for a in (d1, d2, e1, e2)]), lat)
    n = 2 * CH * CH
    gfw, gsw = line[:n].reshape(2, 1, CH, CH), line[n : 2 * n].reshape(2, 1, CH, CH)
    gfb = line[2 * n : 2 * n + 192].reshape(2, 1, CH)
    gsb = line[2 * n + 192 : 2 * n + 384].reshape(2, 1, CH)
    sums2, parts = row_call(
        grad_sums_kernel, "grad_sums", (tokens, upstream, spectral, sums, gain),
        (SUMS, jax.ShapeDtypeStruct((2, CH * LON), f32)), 4,
    )
    sums2 = from_everyone(sums2, "ch")
    grad_tokens = row_call(
        grad_tokens_kernel, "grad_tokens", (tokens, upstream, spectral, sums, sums2, gain), (FIELD,), 4
    )
    ends = jnp.sum(parts.reshape(2 * CH, LON), axis=1)
    ends = from_everyone(ends[None], lat).sum(axis=(0, 1))
    return result, grad_tokens, gfw, gfb, gsw, gsb, ends[:CH], ends[CH:]


def solution(mesh):
    whole, weight, bias = P(None, "lat", "ch"), P(None, "ch", None, None), P(None, "ch", None)
    return jax.shard_map(
        body,
        mesh=mesh,
        in_specs=(whole, P("ch"), P("ch"), weight, bias, weight, bias, whole),
        out_specs=(whole, whole, weight, bias, weight, bias, P("ch"), P("ch")),
        check_vma=False,
    )
```

time: 788 us -> 416 us (0.53); the launches traced: 777 us -> 414 us
  matrix products: 257 us -> 0 us
  local copies, waits for them, and re-layouts: 195 us -> 33.1 us
  Pallas kernels: 0 us -> 90.1 us
  blocking collectives: 17.3 us -> 102 us
  other arithmetic: 59.4 us -> 4.5 us
  waiting for transfers between devices: 187 us -> 136 us
  starting transfers between devices: 58.7 us -> 46.9 us
    dot_general x48 -> x0, matrix products: 257 us -> none  [the longest x24 114 us: block_mix(): return jnp.einsum('bhknc,ncd->bhknd', values, matrix, precision=highest)]
    pallas_call x0 -> x11, Pallas kernels: none -> 90.1 us  [the longest x5 31.9 us: row_call(): pl.pallas_call(kernel, grid=(GROUPS,), in_specs=[spec(x) for x in ins], o...]
    all_gather x0 -> x1, blocking collectives: none -> 84.5 us  [reduced(): return lax.all_gather(mine, axes, axis=0, tiled=True).reshape(-1)]
    convert_element_type x6 -> x0, local copies, waits for them, and re-layouts: 56.6 us -> none  [the longest x1 12.2 us: body(): normed_grad = grad_out + spectral_grad.astype(jnp.float32)]
    another operation x6 -> x0, local copies, waits for them, and re-layouts: 52.3 us -> none  [the longest x4 28.6 us: moved_by_axis(): parts = parts.reshape(*dims, *parts.shape[1:])]
    all_to_all x8 -> x7, waiting for transfers between devices: 187 us -> 136 us  [exchange(): return lax.all_to_all(x, axes, 0, 0, tiled=True)]
    reduce_sum x9 -> x3, other arithmetic: 39.4 us -> 0.27 us  [the longest x1 0.11 us: reduced(): mine = exchange(line.reshape(peers, 1, size), axes).sum(axis=0)]
    mul x6 -> x0, local copies, waits for them, and re-layouts: 20.5 us -> none  [the longest x2 10.3 us: body(): standard = (as_float - center) * inv_scale]
  transfers between devices with their start and end apart: 8 -> 7, of which waited for: 4 -> 6; matrix products, arithmetic and copies ran while one was open for 34% -> 3% of each run, Pallas kernels for 0% -> 10%
where the time goes in v1:
time: 416 us; the launch traced here: 414 us
  waiting for transfers between devices  136 us (33%)
  blocking collectives  102 us (25%)
  Pallas kernels  90.1 us (22%)
  starting transfers between devices  46.9 us (11%)
  local copies, waits for them, and re-layouts  33.1 us (8%)
  other arithmetic  4.5 us (1%)
    all_to_all x7, waiting for transfers between devices, exchange(): return lax.all_to_all(x, axes, 0, 0, tiled=True)  136 us
    all_gather x1, blocking collectives, reduced(): return lax.all_gather(mine, axes, axis=0, tiled=True).reshape(-1)  84.5 us
    all_to_all x7, starting transfers between devices, exchange(): return lax.all_to_all(x, axes, 0, 0, tiled=True)  46.9 us
    pallas_call x5, Pallas kernels, row_call(): pl.pallas_call(kernel, grid=(GROUPS,), in_specs=[spec(x) for x in ins], o...  31.9 us
    unnamed x80, local copies, waits for them, and re-layouts  24.1 us
    all_to_all x1, blocking collectives, exchange(): return lax.all_to_all(x, axes, 0, 0, tiled=True)  17.7 us
    pallas_call x2, Pallas kernels, to_field(): pl.pallas_call(to_field_kernel, grid=(GROUPS,), in_specs=[spec, spec, ful...  17.3 us
    pallas_call x2, Pallas kernels, to_spectrum(): pl.pallas_call(to_spectrum_kernel, grid=(GROUPS,), in_specs=[pl.BlockSpec...  14.6 us
  transfers between devices with their start and end apart: 7, of which 6 were waited for; matrix products, arithmetic and copies ran while one was open for 3% of the time, Pallas kernels for 10%

profile of v1, /device:TPU:1, one launch (start us, length us, event | category | flops | bytes accessed | tf_op | source)
XLA Modules:
  0.0 414.1 jit_solution(5734070382303930408)
XLA Ops:
  2.3 3.4 norm_sums.1
  5.8 17.7 %all_to_all.40.sums_ref = f32[8,64,384]{2,1,0:T(8,128)S(1)} all-to-all(f32[8,64,384]{2,1,0:T(8,128)S(1)} %broadcast_in_dim.10), channel_id=1, replica_groups=mesh['lat'=32,'ch'=8] {'ch'}, dimensions={0} | all-to-all | bytes 1572864 | tf_op jit(solution)/shard_map/all_to_all | solution.py:430
  23.4 12.8 %all-to-all-start.3 = ((bf16[32,2,17280]{2,1,0:T(2,128)(2,1)}), bf16[32,2,17280]{2,1,0:T(2,128)(2,1)S(1)}, u32[]{:S(2)}, u32[]{:S(2)}) async-start(bf16[32,2,17280]{2,1,0:T(2,128)(2,1)} %u_ref.3), calls=%async_computation.3 | async-start | bytes 4423680 | tf_op jit(solution)/shard_map/all_to_all | solution.py:430
  38.4 4.5 %normalize.1.n_ref = bf16[32,2,17280]{2,1,0:T(2,128)(2,1)} custom-call(bf16[32,2,17280]{2,1,0:T(2,128)(2,1)S(1)} %copy-done.6, f32[8,64,384]{2,1,0:T(8,128)S(1)} %all_to_all.40.sums_ref, f32[1,17280]{1,0:T(1,128)S(1)} %reshape.69.gain_ref, f32[1,17280]{1,0:T(1,128)S(1)} %reshape.70.shift_ref), custom_call_target="tpu_custom_call" | custom-call | flops 3000000000 | bytes 8000000 | tf_op jit(solution)/shard_map/normalize/pallas_call | solution.py:412
  43.0 46.4 %all-to-all-done.3.x_ref = bf16[32,2,17280]{2,1,0:T(2,128)(2,1)S(1)} async-done(((bf16[32,2,17280]{2,1,0:T(2,128)(2,1)}), bf16[32,2,17280]{2,1,0:T(2,128)(2,1)S(1)}, u32[]{:S(2)}, u32[]{:S(2)}) %all-to-all-start.3) | async-done | bytes 2211872 | tf_op jit(solution)/shard_map/all_to_all | solution.py:430
  89.4 5.7 %all-to-all-start.1 = ((bf16[32,2,17280]{2,1,0:T(2,128)(2,1)}), bf16[32,2,17280]{2,1,0:T(2,128)(2,1)}, u32[]{:S(2)}, u32[]{:S(2)}) async-start(bf16[32,2,17280]{2,1,0:T(2,128)(2,1)} %normalize.1.n_ref), calls=%async_computation.1 | async-start | bytes 4423680 | tf_op jit(solution)/shard_map/all_to_all | solution.py:430
  105.1 6.8 %to_spectrum.3 = (f32[64,96,128]{2,1,0:T(8,128)S(1)}, f32[64,96,128]{2,1,0:T(8,128)}) custom-call(bf16[32,2,17280]{2,1,0:T(2,128)(2,1)S(1)} %all-to-all-done.3.x_ref, bf16[128,64]{1,0:T(8,128)(2,1)S(1)} %copy-done.18, bf16[256,256]{1,0:T(8,128)(2,1)S(1)} %copy-done.16, bf16[256,256]{1,0:T(8,128)(2,1)S(1)} %copy-done.17), custom_call_target="tpu_custom_call" | custom-call | flops 8000000000 | bytes 9000000 | tf_op jit(solution)/shard_map/to_spectrum/pallas_call | solution.py:105
  113.6 34.9 %all-to-all-done.1.x_ref = bf16[32,2,17280]{2,1,0:T(2,128)(2,1)} async-done(((bf16[32,2,17280]{2,1,0:T(2,128)(2,1)}), bf16[32,2,17280]{2,1,0:T(2,128)(2,1)}, u32[]{:S(2)}, u32[]{:S(2)}) %all-to-all-start.1) | async-done | bytes 2211872 | tf_op jit(solution)/shard_map/all_to_all | solution.py:430
  150.3 7.7 %to_spectrum.2 = (f32[64,96,128]{2,1,0:T(8,128)S(1)}, f32[64,96,128]{2,1,0:T(8,128)}) custom-call(bf16[32,2,17280]{2,1,0:T(2,128)(2,1)} %all-to-all-done.1.x_ref, bf16[128,64]{1,0:T(8,128)(2,1)S(1)} %copy-done.18, bf16[256,256]{1,0:T(8,128)(2,1)S(1)} %copy-done.14, bf16[256,256]{1,0:T(8,128)(2,1)S(1)} %copy-done.15), custom_call_target="tpu_custom_call" | custom-call | flops 8000000000 | bytes 9000000 | tf_op jit(solution)/shard_map/to_spectrum/pallas_call | solution.py:105
  159.7 14.3 %mlp_forward.1 = (f32[64,96,128]{2,1,0:T(8,128)S(1)}, f32[64,96,128]{2,1,0:T(8,128)}, bf16[8,192,1024]{2,1,0:T(8,128)(2,1)}, bf16[8,192,1024]{2,1,0:T(8,128)(2,1...) custom-call(f32[64,96,128]{2,1,0:T(8,128)} %copy-done.26, f32[64,96,128]{2,1,0:T(8,128)} %get-tuple-element.27.im_ref, ...), custom_call_target="tpu_custom_call" | custom-call | flops 8000000000 | bytes 24000000 | tf_op jit(solution)/shard_map/mlp_forward/pallas_call | solution.py:211
  175.7 12.1 %mlp_backward.1 = (f32[64,96,128]{2,1,0:T(8,128)S(1)}, f32[64,96,128]{2,1,0:T(8,128)}, f32[2,96,96]{2,1,0:T(8,128)S(1)}, f32[192,1]{1,0:T(8,128)S(1)}, f32[2,96,96]{2,1,0:T(8,128)S(1)}, /*index=5*/f32[192,1]{1,0:T(8,128)S(1)}) custom-call(f32[64,96,128]{2,1,0:T(8,128)} %copy-done.21, f32[64,96,128]{2,1,0:T(8,128)} %get-tuple-element.31.im_ref, ...), custom_call_target="tpu_custom_call" | custom-call | flops 8000000000 | bytes 24000000 | tf_op jit(solution)/shard_map/mlp_backward/pallas_call | solution.py:266
  190.8 5.7 %all-to-all-start.6 = ((f32[32,1,1280]{2,1,0:T(1,128)}), f32[32,1,1280]{2,1,0:T(1,128)S(1)}, u32[]{:S(2)}, u32[]{:S(2)}) async-start(f32[32,1,1280]{2,1,0:T(1,128)} %bitcast.6), calls=%async_computation.6 | async-start | bytes 327680 | tf_op jit(solution)/shard_map/all_to_all | solution.py:430
  198.4 8.6 %to_field.3 = bf16[32,2,17280]{2,1,0:T(2,128)(2,1)} custom-call(f32[64,96,128]{2,1,0:T(8,128)S(1)} %copy-done.23, f32[64,96,128]{2,1,0:T(8,128)} %get-tuple-element.37.im_ref, bf16[64,64]{1,0:T(8,128)(2,1)S(1)} %copy-done.19, bf16[64,64]{1,0:T(8,128)(2,1)S(1)} %copy-done.20, bf16[256,256]{1,0:T(8,128)(2,1)S(1)} %copy-done.12, bf16[256,256]{1,0:T(8,128)(2,1)S(1)} %copy-done.13), custom_call_target="tpu_custom_call" | custom-call | flops 8000000000 | bytes 9000000 | tf_op jit(solution)/shard_map/to_field/pallas_call | solution.py:146
  207.5 9.6 %all-to-all-start.4 = ((bf16[32,2,17280]{2,1,0:T(2,128)(2,1)}), bf16[32,2,17280]{2,1,0:T(2,128)(2,1)}, u32[]{:S(2)}, u32[]{:S(2)}) async-start(bf16[32,2,17280]{2,1,0:T(2,128)(2,1)} %to_field.3), calls=%async_computation.4 | async-start | bytes 4423680 | tf_op jit(solution)/shard_map/all_to_all | solution.py:430
  219.0 8.6 %to_field.2 = bf16[32,2,17280]{2,1,0:T(2,128)(2,1)} custom-call(f32[64,96,128]{2,1,0:T(8,128)S(1)} %copy-done.25, f32[64,96,128]{2,1,0:T(8,128)} %get-tuple-element.29.im_ref, bf16[64,64]{1,0:T(8,128)(2,1)S(1)} %copy-done.19, bf16[64,64]{1,0:T(8,128)(2,1)S(1)} %copy-done.20, bf16[256,256]{1,0:T(8,128)(2,1)S(1)} %copy-done.10, bf16[256,256]{1,0:T(8,128)(2,1)S(1)} %copy-done.11), custom_call_target="tpu_custom_call" | custom-call | flops 8000000000 | bytes 9000000 | tf_op jit(solution)/shard_map/to_field/pallas_call | solution.py:146
  227.6 42.7 %all-to-all-done.4.s_ref = bf16[32,2,17280]{2,1,0:T(2,128)(2,1)} async-done(((bf16[32,2,17280]{2,1,0:T(2,128)(2,1)}), bf16[32,2,17280]{2,1,0:T(2,128)(2,1)}, u32[]{:S(2)}, u32[]{:S(2)}) %all-to-all-start.4) | async-done | bytes 2211872 | tf_op jit(solution)/shard_map/all_to_all | solution.py:430
  270.3 5.7 %all-to-all-start.2 = ((bf16[32,2,17280]{2,1,0:T(2,128)(2,1)}), bf16[32,2,17280]{2,1,0:T(2,128)(2,1)}, u32[]{:S(2)}, u32[]{:S(2)}) async-start(bf16[32,2,17280]{2,1,0:T(2,128)(2,1)} %to_field.2), calls=%async_computation.2 | async-start | bytes 4423680 | tf_op jit(solution)/shard_map/all_to_all | solution.py:430
  276.1 84.5 %all-gather.1 = f32[32,1,1280]{2,1,0:T(1,128)S(1)} all-gather(f32[1,1,1280]{2,1,0:T(1,128)S(1)} %reshape.88), channel_id=2, replica_groups=mesh['lat'=32,'ch'=8] {'lat'}, dimensions={0}, use_global_device_ids=true | all-gather | bytes 168960 | tf_op jit(solution)/shard_map/all_gather | solution.py:443
  362.3 9.0 %grad_sums.1 = (f32[64,384]{1,0:T(8,128)S(1)}, f32[2,17280]{1,0:T(2,128)S(1)}) custom-call(bf16[32,2,17280]{2,1,0:T(2,128)(2,1)S(1)} %copy-done.7, bf16[32,2,17280]{2,1,0:T(2,128)(2,1)} %u_ref.3, bf16[32,2,17280]{2,1,0:T(2,128)(2,1)} %all-to-all-done.4.s_ref, f32[8,64,384]{2,1,0:T(8,128)S(1)} %all_to_all.40.sums_ref, f32[1,17280]{1,0:T(1,128)S(1)} %copy-done.4), custom_call_target="tpu_custom_call" | custom-call | flops 3000000000 | bytes 8000000 | tf_op jit(solution)/shard_map/grad_sums/pallas_call | solution.py:412
  372.4 3.7 all-to-all-start.7
  376.8 8.8 %all-to-all-done.7 = f32[32,1,192]{2,1,0:T(1,128)S(1)} async-done(((f32[32,1,192]{2,1,0:T(1,128)}), f32[32,1,192]{2,1,0:T(1,128)S(1)}, u32[]{:S(2)}, u32[]{:S(2)}) %all-to-all-start.7) | async-done | bytes 24608 | tf_op jit(solution)/shard_map/all_to_all | solution.py:430
  386.5 3.8 all-to-all-start.5
  394.0 5.5 %result.1 = bf16[32,2,17280]{2,1,0:T(2,128)(2,1)} custom-call(bf16[32,2,17280]{2,1,0:T(2,128)(2,1)S(1)} %copy-done.8, bf16[32,2,17280]{2,1,0:T(2,128)(2,1)} %normalize.1.n_ref, bf16[32,2,17280]{2,1,0:T(2,128)(2,1)} %all-to-all-done.2.f_ref), custom_call_target="tpu_custom_call" | custom-call | flops 3000000000 | bytes 8000000 | tf_op jit(solution)/shard_map/result/pallas_call | solution.py:412
  404.7 9.5 %grad_tokens.1 = bf16[32,2,17280]{2,1,0:T(2,128)(2,1)} custom-call(bf16[32,2,17280]{2,1,0:T(2,128)(2,1)S(1)} %copy-done.9, bf16[32,2,17280]{2,1,0:T(2,128)(2,1)} %u_ref.3, bf16[32,2,17280]{2,1,0:T(2,128)(2,1)} %all-to-all-done.4.s_ref, f32[8,64,384]{2,1,0:T(8,128)S(1)} %all_to_all.40.sums_ref, f32[8,64,384]{2,1,0:T(8,128)S(1)} %all-to-all-done.5.grads_ref, ...), custom_call_target="tpu_custom_call" | custom-call | flops 3000000000 | bytes 8000000 | tf_op jit(solution)/shard_map/grad_tokens/pallas_call | solution.py:412
  (120 shorter events, 41.0 us)
Async XLA Ops:
  5.7 30.5 %copy-start.37 = (f32[96]{0:T(128)S(1)}, f32[96]{0:T(128)}, u32[]{:S(2)}) copy-start(f32[96]{0:T(128)} %param.23) | copy-start | bytes 1156
  5.7 30.8 %copy-start.38 = (f32[96]{0:T(128)S(1)}, f32[96]{0:T(128)}, u32[]{:S(2)}) copy-start(f32[96]{0:T(128)} %param.24) | copy-start | bytes 1156
  23.4 66.0 %all-to-all-start.3 = ((bf16[32,2,17280]{2,1,0:T(2,128)(2,1)}), bf16[32,2,17280]{2,1,0:T(2,128)(2,1)S(1)}, u32[]{:S(2)}, u32[]{:S(2)}) async-start(bf16[32,2,17280]{2,1,0:T(2,128)(2,1)} %u_ref.3), calls=%async_computation.3 | async-start | bytes 4423680 | tf_op jit(solution)/shard_map/all_to_all | solution.py:430
  43.0 52.2 %copy-start.33 = (f32[2,1,96,96]{3,2,1,0:T(8,128)S(1)}, f32[2,1,96,96]{3,2,1,0:T(8,128)}, u32[]{:S(2)}) copy-start(f32[2,1,96,96]{3,2,1,0:T(8,128)} %param.25) | copy-start | bytes 221188
  43.0 53.6 %copy-start.35 = (f32[2,1,96]{2,1,0:T(1,128)S(1)}, f32[2,1,96]{2,1,0:T(1,128)}, u32[]{:S(2)}) copy-start(f32[2,1,96]{2,1,0:T(1,128)} %param.26) | copy-start | bytes 2308
  43.0 54.5 %copy-start.34 = (f32[2,1,96,96]{3,2,1,0:T(8,128)S(1)}, f32[2,1,96,96]{3,2,1,0:T(8,128)}, u32[]{:S(2)}) copy-start(f32[2,1,96,96]{3,2,1,0:T(8,128)} %param.27) | copy-start | bytes 221188
  43.0 57.0 %copy-start.36 = (f32[2,1,96]{2,1,0:T(1,128)S(1)}, f32[2,1,96]{2,1,0:T(1,128)}, u32[]{:S(2)}) copy-start(f32[2,1,96]{2,1,0:T(1,128)} %param.28) | copy-start | bytes 2308
  43.0 60.2 %copy-start.18 = (bf16[128,64]{1,0:T(8,128)(2,1)S(1)}, bf16[128,64]{1,0:T(8,128)(2,1)}, u32[]{:S(2)}) copy-start(bf16[128,64]{1,0:T(8,128)(2,1)} %constant.26.clone.lat_ref) | copy-start | bytes 49156
  89.4 59.1 %all-to-all-start.1 = ((bf16[32,2,17280]{2,1,0:T(2,128)(2,1)}), bf16[32,2,17280]{2,1,0:T(2,128)(2,1)}, u32[]{:S(2)}, u32[]{:S(2)}) async-start(bf16[32,2,17280]{2,1,0:T(2,128)(2,1)} %normalize.1.n_ref), calls=%async_computation.1 | async-start | bytes 4423680 | tf_op jit(solution)/shard_map/all_to_all | solution.py:430
  113.6 46.1 %copy-start = (f32[192,1]{1,0:T(8,128)S(1)}, f32[192,1]{1,0:T(8,128)}, u32[]{:S(2)}) copy-start(f32[192,1]{1,0:T(8,128)} %reshape.91.b2_ref) | copy-start | bytes 2308
  159.7 16.0 %copy-start.1 = (bf16[192,192]{1,0:T(8,128)(2,1)S(1)}, bf16[192,192]{1,0:T(8,128)(2,1)}, u32[]{:S(2)}) copy-start(bf16[192,192]{1,0:T(8,128)(2,1)} %get-tuple-element.54.w2_ref) | copy-start | bytes 221188
  159.7 16.0 %copy-start.2 = (bf16[192,192]{1,0:T(8,128)(2,1)S(1)}, bf16[192,192]{1,0:T(8,128)(2,1)}, u32[]{:S(2)}) copy-start(bf16[192,192]{1,0:T(8,128)(2,1)} %get-tuple-element.55.w1_ref) | copy-start | bytes 221188
  175.7 20.8 %copy-start.12 = (bf16[256,256]{1,0:T(8,128)(2,1)S(1)}, bf16[256,256]{1,0:T(8,128)(2,1)}, u32[]{:S(2)}) copy-start(bf16[256,256]{1,0:T(8,128)(2,1)} %constant.35.clone.lonh_ref) | copy-start | bytes 393220
  175.7 20.8 %copy-start.13 = (bf16[256,256]{1,0:T(8,128)(2,1)S(1)}, bf16[256,256]{1,0:T(8,128)(2,1)}, u32[]{:S(2)}) copy-start(bf16[256,256]{1,0:T(8,128)(2,1)} %constant.36.clone.lonl_ref) | copy-start | bytes 393220
  175.7 20.8 %copy-start.19 = (bf16[64,64]{1,0:T(8,128)(2,1)S(1)}, bf16[64,64]{1,0:T(8,128)(2,1)}, u32[]{:S(2)}) copy-start(bf16[64,64]{1,0:T(8,128)(2,1)} %constant.31.clone.lath_ref) | copy-start | bytes 24580
  175.7 20.8 %copy-start.20 = (bf16[64,64]{1,0:T(8,128)(2,1)S(1)}, bf16[64,64]{1,0:T(8,128)(2,1)}, u32[]{:S(2)}) copy-start(bf16[64,64]{1,0:T(8,128)(2,1)} %constant.32.clone.latl_ref) | copy-start | bytes 24580
  190.8 16.7 %all-to-all-start.6 = ((f32[32,1,1280]{2,1,0:T(1,128)}), f32[32,1,1280]{2,1,0:T(1,128)S(1)}, u32[]{:S(2)}, u32[]{:S(2)}) async-start(f32[32,1,1280]{2,1,0:T(1,128)} %bitcast.6), calls=%async_computation.6 | async-start | bytes 327680 | tf_op jit(solution)/shard_map/all_to_all | solution.py:430
  207.0 10.0 %copy-start.10 = (bf16[256,256]{1,0:T(8,128)(2,1)S(1)}, bf16[256,256]{1,0:T(8,128)(2,1)}, u32[]{:S(2)}) copy-start(bf16[256,256]{1,0:T(8,128)(2,1)} %constant.33.clone.lonh_ref) | copy-start | bytes 393220
  207.0 10.0 %copy-start.11 = (bf16[256,256]{1,0:T(8,128)(2,1)S(1)}, bf16[256,256]{1,0:T(8,128)(2,1)}, u32[]{:S(2)}) copy-start(bf16[256,256]{1,0:T(8,128)(2,1)} %constant.34.clone.lonl_ref) | copy-start | bytes 393220
  207.5 62.8 %all-to-all-start.4 = ((bf16[32,2,17280]{2,1,0:T(2,128)(2,1)}), bf16[32,2,17280]{2,1,0:T(2,128)(2,1)}, u32[]{:S(2)}, u32[]{:S(2)}) async-start(bf16[32,2,17280]{2,1,0:T(2,128)(2,1)} %to_field.3), calls=%async_computation.4 | async-start | bytes 4423680 | tf_op jit(solution)/shard_map/all_to_all | solution.py:430
  227.6 133.1 %copy-start.4 = (f32[1,17280]{1,0:T(1,128)S(1)}, f32[1,17280]{1,0:T(1,128)}, u32[]{:S(2)}) copy-start(f32[1,17280]{1,0:T(1,128)} %copy-done.3) | copy-start | bytes 207364
  270.3 101.4 %all-to-all-start.2 = ((bf16[32,2,17280]{2,1,0:T(2,128)(2,1)}), bf16[32,2,17280]{2,1,0:T(2,128)(2,1)}, u32[]{:S(2)}, u32[]{:S(2)}) async-start(bf16[32,2,17280]{2,1,0:T(2,128)(2,1)} %to_field.2), calls=%async_computation.2 | async-start | bytes 4423680 | tf_op jit(solution)/shard_map/all_to_all | solution.py:430
  372.4 13.2 %all-to-all-start.7 = ((f32[32,1,192]{2,1,0:T(1,128)}), f32[32,1,192]{2,1,0:T(1,128)S(1)}, u32[]{:S(2)}, u32[]{:S(2)}) async-start(f32[32,1,192]{2,1,0:T(1,128)} %broadcast_in_dim.14), calls=%async_computation.7 | async-start | bytes 65536 | tf_op jit(solution)/shard_map/all_to_all | solution.py:430
  386.5 16.6 %all-to-all-start.5 = ((f32[8,64,384]{2,1,0:T(8,128)}), f32[8,64,384]{2,1,0:T(8,128)S(1)}, u32[]{:S(2)}, u32[]{:S(2)}) async-start(f32[8,64,384]{2,1,0:T(8,128)} %broadcast_in_dim.13), calls=%async_computation.5 | async-start | bytes 1572864 | tf_op jit(solution)/shard_map/all_to_all | solution.py:430
  (22 other events, 32.5 us)

commit v2 on v0

v2 whole, which is shorter than its diff:
```python
import functools
import math

import jax
import jax.numpy as jnp
import numpy as np
from jax import lax
from jax.experimental import pallas as pl
from jax.experimental.pallas import tpu as pltpu
from jax.sharding import Mesh
from jax.sharding import PartitionSpec as P

LAT_ROWS = 64
LON = 180
MODES = 91
CH = 96
GROUP = 32
GROUPS = CH // GROUP
SPAN = GROUP * LON
PITCH = 40
EMBED = 768
layer_eps = 1e-05
shrink = 0.1
f32 = jnp.float32
bf16 = jnp.bfloat16


def split_table(table):
    high = table.astype(np.float32).astype(bf16)
    low = (table - high.astype(np.float64)).astype(np.float32).astype(bf16)
    return high, low


@functools.cache
def tables():
    m = np.arange(33)[:, None]
    h = np.arange(LAT_ROWS)[None, :]
    ang = 2.0 * np.pi * ((m * h) % LAT_ROWS) / LAT_ROWS
    lat = np.concatenate([np.cos(ang), np.sin(ang)[1:32]], axis=0) / math.sqrt(LAT_ROWS)
    w = np.arange(LON)[:, None]
    k = np.arange(MODES)[None, :]
    ang = 2.0 * np.pi * ((w * k) % LON) / LON
    lon = np.zeros((256, 256))
    lon[:LON, :MODES] = np.cos(ang) / math.sqrt(LON)
    lon[:LON, 128 : 128 + MODES] = np.sin(ang) / math.sqrt(LON)
    lon[:LON, 128 + MODES - 1] = 0.0
    lon[:LON, 128] = 0.0
    double = np.zeros((256,))
    double[:MODES] = 2.0
    double[128 : 128 + MODES] = 2.0
    double[[0, MODES - 1, 128, 128 + MODES - 1]] = 1.0
    return lat, lon, lon * double[None, :]


def split(x):
    high = x.astype(bf16)
    return high, (x - high.astype(f32)).astype(bf16)


def dot(a, b):
    return jnp.dot(a, b, preferred_element_type=f32)


def dot_nt(a, b):
    return lax.dot_general(a, b, (((1,), (1,)), ((), ())), preferred_element_type=f32)


STEP = 8


def gather_modes(re, im):
    return jnp.concatenate([jnp.concatenate([re[j], im[j]], axis=0) for j in range(STEP)], axis=1)


def big_matrix(weight):
    real, imag = weight[0, 0], weight[1, 0]
    return jnp.block([[real, imag], [-imag, real]])


def lane_parts(ref_or_value):
    return [slice(c * LON, (c + 1) * LON) for c in range(GROUP)]


def widen(dst, values):
    for part in lane_parts(dst):
        dst[:, part] = values


def narrow(src):
    total = None
    for part in lane_parts(src):
        v = src[:, part]
        total = v if total is None else total + v
    return total


MESH = pl.DeviceIdType.MESH
UP, NORM, FILT, GRAD = range(4)


def mega_kernel(
    tokens, upstream, gain_ref, shift_ref, w1_ref, b1_ref, w2_ref, b2_ref,
    lat_ref, lonh, lonl, latih, latil, lonih, lonil,
    result, grad_tokens, params_out, ends_out,
    tok, upr, cols, normed, filt, grad, spec, stash, zs, ya, yb, center, scale, first, second,
    sums_send, sums_recv, wh, wl, wt, a1, a2, c1, c2, pack, packed_recv, piece, parts, ends_send, ends_recv,
    load_sem, store_sem, send_sem, recv_sem, ch_send, ch_recv, small_send, small_recv,
):
    lat = lax.axis_index("lat")
    ch = lax.axis_index("ch")
    peers, chs = 32, 8

    def peer_at(s):
        return lax.rem(lat + 64 + ((s + 1) // 2) * (2 * lax.rem(s, 2) - 1), peers)

    def lanes(g):
        return pl.ds(pl.multiple_of(g * SPAN, SPAN), SPAN)

    def each_peer(fn):
        lax.fori_loop(1, peers, lambda s, z: (fn(peer_at(s)), z)[1], 0)

    def each_ch(fn):
        lax.fori_loop(1, chs, lambda s, z: (fn(lax.rem(ch + s, chs)), z)[1], 0)

    loads = [
        pltpu.make_async_copy(upstream, upr, load_sem.at[0]),
        pltpu.make_async_copy(tokens, tok, load_sem.at[1]),
    ]
    for c in loads:
        c.start()

    barrier = pltpu.get_barrier_semaphore()
    each_peer(lambda p: pl.semaphore_signal(barrier, inc=1, device_id={"lat": p}, device_id_type=MESH))
    each_ch(lambda p: pl.semaphore_signal(barrier, inc=1, device_id={"ch": p}, device_id_type=MESH))
    pl.semaphore_wait(barrier, peers - 1 + chs - 1)

    def send_field(src, dst, kind, g):
        def go(p):
            pltpu.make_async_remote_copy(
                src_ref=src.at[p, :, lanes(g)],
                dst_ref=dst.at[lat, :, lanes(g)],
                send_sem=send_sem.at[kind, g],
                recv_sem=recv_sem.at[kind, g],
                device_id={"lat": p},
                device_id_type=MESH,
            ).start()

        each_peer(go)

    def wait_bytes(buf, sem):
        ref = buf.at[pl.ds(0, peers - 1)]
        pltpu.make_async_copy(ref, ref, sem).wait()

    def wait_field(buf, sem, kind, g):
        ref = buf.at[pl.ds(0, peers - 1), :, lanes(g)]
        pltpu.make_async_copy(ref, ref, sem.at[kind, g]).wait()

    def keep_own(src, dst, g):
        dst[lat, :, lanes(g)] = src[lat, :, lanes(g)]

    loads[0].wait()
    send_field(upr, cols.at[0], UP, 0)
    send_field(upr, cols.at[0], UP, 1)
    loads[1].wait()

    def rows_of(ref, g):
        return ref[:, :, lanes(g)].reshape(LAT_ROWS, SPAN).astype(f32)

    def put_rows(ref, g, value):
        ref[:, :, lanes(g)] = value.astype(bf16).reshape(32, 2, SPAN)

    def over_channels(which):
        sums_send[which, :, 0:LON] = narrow(first)
        sums_send[which, :, LON : 2 * LON] = narrow(second)
        sums_send[which, :, 2 * LON :] = jnp.zeros((LAT_ROWS, 384 - 2 * LON), f32)
        sums_recv[which, ch] = sums_send[which]

        def go(p):
            pltpu.make_async_remote_copy(
                src_ref=sums_send.at[which],
                dst_ref=sums_recv.at[which, ch],
                send_sem=ch_send.at[which],
                recv_sem=ch_recv.at[which],
                device_id={"ch": p},
                device_id_type=MESH,
            ).start()

        each_ch(go)

    def wait_channels(which):
        ref = sums_recv.at[which, pl.ds(0, chs - 1)]
        pltpu.make_async_copy(ref, ref, ch_recv.at[which]).wait()
        total = sums_recv[which, 0]
        for p in range(1, chs):
            total = total + sums_recv[which, p]
        return total * (1.0 / EMBED)

    first[...] = jnp.zeros_like(first)
    second[...] = jnp.zeros_like(second)

    @pl.loop(0, GROUPS)
    def _(g):
        x = rows_of(tok, g)
        first[...] += x
        second[...] += x * x

    over_channels(0)
    ya[...] = jnp.zeros_like(ya)
    yb[...] = jnp.zeros_like(yb)
    wh[0], wl[0] = split(w1_ref[...].T)
    wh[1], wl[1] = split(w2_ref[...].T)
    wt[0] = w1_ref[...].astype(bf16)
    wt[1] = w2_ref[...].astype(bf16)
    for g in range(GROUPS):
        keep_own(upr, cols.at[0], g)
    for r in (a1, a2, c1, c2):
        r[...] = jnp.zeros_like(r)
    sums = wait_channels(0)
    mean = sums[:, 0:LON]
    variance = sums[:, LON : 2 * LON] - mean * mean
    widen(center, mean)
    widen(scale, lax.rsqrt(variance + layer_eps))

    @pl.loop(0, GROUPS)
    def _(g):
        standard = (rows_of(tok, g) - center[...]) * scale[...]
        put_rows(normed, g, standard * gain_ref[:, lanes(g)] + shift_ref[:, lanes(g)])
        keep_own(normed, cols.at[1], g)
        send_field(normed, cols.at[1], NORM, g)

    send_field(upr, cols.at[0], UP, 2)

    def spectrum(field, g):
        x = cols[field, :, :, lanes(g)].reshape(LAT_ROWS, SPAN)
        both = dot(lat_ref[...], x)
        zs[...] = both[:LAT_ROWS] + both[LAT_ROWS:]
        for c in range(GROUP):
            v = zs[:, c * LON : (c + 1) * LON]
            ya[pl.ds(c, LAT_ROWS, stride=PITCH), :] = v[:, :128]
            yb[pl.ds(c, LAT_ROWS, stride=PITCH), 0 : LON - 128] = v[:, 128:]
        rows = jnp.concatenate([ya[...], yb[...]], axis=1)
        rows = rows.reshape(LAT_ROWS, PITCH, 256)[:, :GROUP].reshape(LAT_ROWS * GROUP, 256)
        high, low = split(rows)
        p = dot(high, lonh[field]) + dot(low, lonh[field]) + dot(high, lonl[field])
        p = p.reshape(LAT_ROWS, GROUP, 256)
        cc, cs = p[:, :, :128], p[:, :, 128:]
        here = pl.ds(pl.multiple_of(g * GROUP, GROUP), GROUP)
        re, im = spec.at[field, 0], spec.at[field, 1]
        re[0:1, here] = cc[0:1]
        im[0:1, here] = -cs[0:1]
        re[32:33, here] = cc[32:33]
        im[32:33, here] = -cs[32:33]
        re[1:32, here] = cc[1:32] - cs[33:64]
        re[33:64, here] = cc[1:32] + cs[33:64]
        im[1:32, here] = -cs[1:32] - cc[33:64]
        im[33:64, here] = cc[33:64] - cs[1:32]

    @pl.loop(0, 2)
    def _(g):
        wait_field(cols.at[0], recv_sem, UP, g)
        spectrum(0, g)

    @pl.loop(0, GROUPS)
    def _(g):
        wait_field(cols.at[1], recv_sem, NORM, g)
        spectrum(1, g)

    @pl.loop(0, LAT_ROWS // STEP)
    def _(i):
        at = pl.ds(i * STEP, STEP)
        re, im = spec.at[1, 0], spec.at[1, 1]
        xh, xl = split(gather_modes(re[at], im[at]))
        pre = dot(wh[0], xh) + dot(wh[0], xl) + dot(wl[0], xh) + b1_ref[...]
        a = math.sqrt(2.0 / math.pi)
        sq = pre * pre
        th = jnp.tanh(a * pre * (1.0 + 0.044715 * sq))
        half = 0.5 * (1.0 + th)
        hid = pre * half
        slope = half + 0.5 * pre * (1.0 - th * th) * (a * (1.0 + 3.0 * 0.044715 * sq))
        hh, hl = split(hid)
        pre2 = dot(wh[1], hh) + dot(wh[1], hl) + dot(wl[1], hh) + b2_ref[...]
        t = jnp.tanh(pre2 * (1.0 / shrink))
        mixed = pre2 - shrink * t
        for j in range(STEP):
            re[i * STEP + j] = mixed[:CH, 128 * j : 128 * (j + 1)]
            im[i * STEP + j] = mixed[CH:, 128 * j : 128 * (j + 1)]
        stash[0, i] = xh
        stash[1, i] = slope.astype(bf16)
        stash[2, i] = hh
        stash[3, i] = (t * t).astype(bf16)

    def field_of(field, g, dst):
        here = pl.ds(pl.multiple_of(g * GROUP, GROUP), GROUP)
        gr, gi = spec[field, 0, :, here], spec[field, 1, :, here]
        left = jnp.concatenate([gr[0:1], gr[1:32] + gr[33:64], gr[32:33], gi[33:64] - gi[1:32]], axis=0)
        right = -jnp.concatenate([gi[0:1], gi[1:32] + gi[33:64], gi[32:33], gr[1:32] - gr[33:64]], axis=0)
        rows = jnp.concatenate([left, right], axis=2).reshape(LAT_ROWS * GROUP, 256).astype(bf16)
        v = dot(rows, lonih[field]) + dot(rows, lonil[field])
        v = v.reshape(LAT_ROWS, GROUP, 256)
        va, vb = ya.reshape(LAT_ROWS, PITCH, 128), yb.reshape(LAT_ROWS, PITCH, 128)
        va[:, 0:GROUP, :] = v[:, :, :128]
        vb[:, 0:GROUP, :] = v[:, :, 128:]
        for c in range(GROUP):
            zs[:, c * LON : c * LON + 128] = ya[pl.ds(c, LAT_ROWS, stride=PITCH), :]
            zs[:, c * LON + 128 : (c + 1) * LON] = yb[pl.ds(c, LAT_ROWS, stride=PITCH), 0 : LON - 128]
        z = zs[...].astype(bf16)
        put_rows(dst, g, dot(latih[...], z) + dot(latil[...], z))

    @pl.loop(0, GROUPS)
    def _(g):
        field_of(1, g, cols.at[1])
        keep_own(cols.at[1], filt, g)
        send_field(cols.at[1], filt, FILT, g)

    wait_field(cols.at[0], recv_sem, UP, 2)
    yb[:, LON - 128 :] = jnp.zeros((LAT_ROWS * PITCH, 256 - LON), f32)
    spectrum(0, 2)

    @pl.loop(0, LAT_ROWS // STEP)
    def _(i):
        at = pl.ds(i * STEP, STEP)
        re, im = spec.at[0, 0], spec.at[0, 1]
        p2 = gather_modes(re[at], im[at]) * stash[3, i].astype(f32)
        p2h = p2.astype(bf16)
        p1 = dot(wt[1], p2h) * stash[1, i].astype(f32)
        p1h = p1.astype(bf16)
        out = dot(wt[0], p1h)
        for j in range(STEP):
            re[i * STEP + j] = out[:CH, 128 * j : 128 * (j + 1)]
            im[i * STEP + j] = out[CH:, 128 * j : 128 * (j + 1)]
        a2[...] += dot_nt(stash[2, i], p2h)
        a1[...] += dot_nt(stash[0, i], p1h)
        c2[...] += sum(p2[:, 128 * j : 128 * (j + 1)] for j in range(STEP))
        c1[...] += sum(p1[:, 128 * j : 128 * (j + 1)] for j in range(STEP))

    @pl.loop(0, GROUPS)
    def _(g):
        field_of(0, g, cols.at[0])
        keep_own(cols.at[0], grad, g)
        send_field(cols.at[0], grad, GRAD, g)

    pack[...] = jnp.zeros_like(pack)
    for n, (acc, line) in enumerate(((a1, c1), (a2, c2))):
        v = acc[...]
        top = n * 2 * CH
        pack[top : top + CH, :CH] = v[:CH, :CH] + v[CH:, CH:]
        pack[top + CH : top + 2 * CH, :CH] = v[:CH, CH:] - v[CH:, :CH]
        pack[top : top + 2 * CH, CH : CH + 1] = jnp.sum(line[...], axis=1, keepdims=True)

    def rows16(p):
        return pl.ds(pl.multiple_of(p * 16, 16), 16)

    packed_recv[lat] = pack[rows16(lat), :]

    def send_piece(p):
        pltpu.make_async_remote_copy(
            src_ref=pack.at[rows16(p), :],
            dst_ref=packed_recv.at[lat],
            send_sem=small_send.at[0],
            recv_sem=small_recv.at[0],
            device_id={"lat": p},
            device_id_type=MESH,
        ).start()

    each_peer(send_piece)

    @pl.loop(0, GROUPS)
    def _(g):
        wait_field(filt, recv_sem, FILT, g)
        put_rows(filt, g, rows_of(tok, g) + rows_of(normed, g) + rows_of(filt, g))
        pltpu.make_async_copy(filt.at[:, :, lanes(g)], result.at[:, :, lanes(g)], store_sem.at[0, g]).start()

    wait_bytes(packed_recv, small_recv.at[0])
    piece[...] = jnp.sum(packed_recv[...], axis=0)
    params_out[lat] = piece[...]

    def send_sum(p):
        pltpu.make_async_remote_copy(
            src_ref=piece,
            dst_ref=params_out.at[lat],
            send_sem=small_send.at[1],
            recv_sem=small_recv.at[1],
            device_id={"lat": p},
            device_id_type=MESH,
        ).start()

    each_peer(send_sum)

    parts[...] = jnp.zeros_like(parts)
    first[...] = jnp.zeros_like(first)
    second[...] = jnp.zeros_like(second)

    @pl.loop(0, GROUPS)
    def _(g):
        wait_field(grad, recv_sem, GRAD, g)
        standard = (rows_of(tok, g) - center[...]) * scale[...]
        total = rows_of(upr, g) + rows_of(grad, g)
        cross = total * standard
        gain = gain_ref[:, lanes(g)]
        first[...] += total * gain
        second[...] += cross * gain
        parts[0:1, lanes(g)] = jnp.sum(cross, axis=0, keepdims=True)
        parts[1:2, lanes(g)] = jnp.sum(total, axis=0, keepdims=True)

    over_channels(1)

    @pl.loop(0, GROUPS)
    def _(g):
        base = parts[:, lanes(g)]
        column = jnp.concatenate(
            [jnp.sum(base[:, c * LON : (c + 1) * LON], axis=1, keepdims=True) for c in range(GROUP)], axis=1
        )
        ends_send[g] = jnp.concatenate([column, jnp.zeros((8, 128 - GROUP), f32)], axis=1)

    ends_recv[lat] = ends_send[...]

    def send_ends(p):
        pltpu.make_async_remote_copy(
            src_ref=ends_send,
            dst_ref=ends_recv.at[lat],
            send_sem=small_send.at[2],
            recv_sem=small_recv.at[2],
            device_id={"lat": p},
            device_id_type=MESH,
        ).start()

    each_peer(send_ends)
    sums = wait_channels(1)
    widen(first, sums[:, 0:LON])
    widen(second, sums[:, LON : 2 * LON])

    @pl.loop(0, GROUPS)
    def _(g):
        inverse = scale[...]
        standard = (rows_of(tok, g) - center[...]) * inverse
        up = rows_of(upr, g)
        slope = (up + rows_of(grad, g)) * gain_ref[:, lanes(g)]
        put_rows(grad, g, up + inverse * (slope - first[...] - standard * second[...]))
        pltpu.make_async_copy(grad.at[:, :, lanes(g)], grad_tokens.at[:, :, lanes(g)], store_sem.at[1, g]).start()

    wait_bytes(ends_recv, small_recv.at[2])
    ends_out[...] = jnp.sum(ends_recv[...], axis=0)
    wait_bytes(params_out, small_recv.at[1])
    for which, buf, out in ((0, filt, result), (1, grad, grad_tokens)):
        for g in range(GROUPS):
            pltpu.make_async_copy(buf.at[:, :, lanes(g)], out.at[:, :, lanes(g)], store_sem.at[which, g]).wait()
    for kind, buf in ((UP, upr), (NORM, normed), (FILT, cols.at[1]), (GRAD, cols.at[0])):
        for g in range(GROUPS):
            wait_field(buf, send_sem, kind, g)
    for which in range(2):
        ref = sums_recv.at[which, pl.ds(0, chs - 1)]
        pltpu.make_async_copy(ref, ref, ch_send.at[which]).wait()
    wait_bytes(packed_recv, small_send.at[0])
    wait_bytes(params_out, small_send.at[1])
    wait_bytes(ends_recv, small_send.at[2])


def mega(tokens, upstream, gain, shift, w1, b1, w2, b2):
    lat, lon, lon2 = tables()
    pair = lambda a, b: [jnp.asarray(np.stack(x)) for x in zip(split_table(a), split_table(b))]
    lat_h, lat_l = split_table(lat)
    lati_h, lati_l = split_table(lat.T)
    lonh, lonl = pair(lon2, lon)
    lonih, lonil = pair(lon.T, lon2.T)
    hbm, vmem = pl.BlockSpec(memory_space=pl.ANY), pl.BlockSpec(memory_space=pltpu.VMEM)
    field = jax.ShapeDtypeStruct((32, 2, CH * LON), bf16)
    V, D = pltpu.VMEM, pltpu.SemaphoreType.DMA
    fld = V((32, 2, CH * LON), bf16)
    wide = V((LAT_ROWS, SPAN), f32)
    ins = [
        tokens, upstream, gain, shift, w1, b1, w2, b2,
        jnp.asarray(np.concatenate([lat_h, lat_l], axis=0)), lonh, lonl,
        jnp.asarray(lati_h), jnp.asarray(lati_l), lonih, lonil,
    ]
    return pl.pallas_call(
        mega_kernel,
        in_specs=[hbm, hbm] + [vmem] * (len(ins) - 2),
        out_specs=[hbm, hbm, vmem, vmem],
        out_shape=[
            field, field,
            jax.ShapeDtypeStruct((32, 16, 128), f32),
            jax.ShapeDtypeStruct((GROUPS, 8, 128), f32),
        ],
        scratch_shapes=[
            fld, fld, V((2, 32, 2, CH * LON), bf16), fld, fld, fld,
            V((2, 2, LAT_ROWS, CH, 128), f32),
            V((4, LAT_ROWS // STEP, 2 * CH, 128 * STEP), bf16),
            wide, V((LAT_ROWS * PITCH, 128), f32), V((LAT_ROWS * PITCH, 128), f32),
            wide, wide, wide, wide,
            V((2, LAT_ROWS, 384), f32), V((2, 8, LAT_ROWS, 384), f32),
            V((2, 192, 192), bf16), V((2, 192, 192), bf16), V((2, 192, 192), bf16),
            V((192, 192), f32), V((192, 192), f32), V((192, 128), f32), V((192, 128), f32),
            V((512, 128), f32), V((32, 16, 128), f32), V((16, 128), f32),
            V((8, CH * LON), f32), V((GROUPS, 8, 128), f32), V((32, GROUPS, 8, 128), f32),
            D((2,)), D((2, GROUPS)), D((4, GROUPS)), D((4, GROUPS)), D((2,)), D((2,)), D((3,)), D((3,)),
        ],
        compiler_params=pltpu.CompilerParams(
            collective_id=0, has_side_effects=True, vmem_limit_bytes=67_043_328
        ),
        name="afno",
    )(*ins)


def body(
    tokens, norm_gain, norm_shift, first_weight, first_bias, second_weight, second_bias, upstream
):
    wide = lambda v: jnp.broadcast_to(v[:, None], (CH, LON)).reshape(1, CH * LON)
    result, grad_tokens, params, ends = mega(
        tokens, upstream, wide(norm_gain), wide(norm_shift),
        big_matrix(first_weight), first_bias.reshape(2 * CH, 1),
        big_matrix(second_weight), second_bias.reshape(2 * CH, 1),
    )
    params = params.reshape(512, 128)[: 4 * CH].reshape(2, 2, 1, CH, 128)
    weights, biases = params[..., :CH], params[..., CH]
    return (
        result, grad_tokens, weights[0], biases[0], weights[1], biases[1],
        ends[:, 0, :GROUP].reshape(CH), ends[:, 1, :GROUP].reshape(CH),
    )


def solution(mesh):
    whole, weight, bias = P(None, "lat", "ch"), P(None, "ch", None, None), P(None, "ch", None)
    return jax.shard_map(
        body,
        mesh=mesh,
        in_specs=(whole, P("ch"), P("ch"), weight, bias, weight, bias, whole),
        out_specs=(whole, whole, weight, bias, weight, bias, P("ch"), P("ch")),
        check_vma=False,
    )
```

time: 788 us -> 270 us (0.34); the launches traced: 777 us -> 269 us
  matrix products: 257 us -> 0 us
  Pallas kernels: 0 us -> 246 us
  waiting for transfers between devices: 187 us -> 0 us
  local copies, waits for them, and re-layouts: 195 us -> 17.9 us
  starting transfers between devices: 58.7 us -> 0 us
  other arithmetic: 59.4 us -> 5.21 us
  blocking collectives: 17.3 us -> 0 us
    dot_general x48 -> x0, matrix products: 257 us -> none  [the longest x24 114 us: block_mix(): return jnp.einsum('bhknc,ncd->bhknd', values, matrix, precision=highest)]
    pallas_call x0 -> x1, Pallas kernels: none -> 246 us  [mega(): pl.pallas_call(mega_kernel, in_specs=[hbm, hbm] + [vmem] * (len(ins) - 2)...]
    all_to_all x8 -> x0, waiting for transfers between devices: 187 us -> none  [the longest x2 96.2 us: from_everyone(): lax.all_to_all(jnp.broadcast_to(x[None], (peers, *x.shape)), axis, 0, 0,...]
    all_to_all x8 -> x0, starting transfers between devices: 58.7 us -> none  [the longest x4 24.3 us: moved_by_axis(): lax.all_to_all(parts, axes[k], split_axis=k, concat_axis=k, tiled=True)]
    convert_element_type x6 -> x0, local copies, waits for them, and re-layouts: 56.6 us -> none  [the longest x1 12.2 us: body(): normed_grad = grad_out + spectral_grad.astype(jnp.float32)]
    another operation x6 -> x2, local copies, waits for them, and re-layouts: 52.3 us -> 1.19 us  [the longest x1 0.59 us: body(): ends[:, 0, :GROUP].reshape(CH)]
    reduce_sum x9 -> x0, other arithmetic: 39.4 us -> none  [the longest x2 17.9 us: channel_sums(): jnp.sum(first_term, axis=-2)]
    mul x6 -> x0, local copies, waits for them, and re-layouts: 20.5 us -> none  [the longest x2 10.3 us: body(): standard = (as_float - center) * inv_scale]
  transfers between devices with their start and end apart: 8 -> 0, of which waited for: 4 -> 0; matrix products, arithmetic and copies ran while one was open for 34% -> 0% of each run, Pallas kernels for 0% -> 0%
where the time goes in v2:
time: 270 us; the launch traced here: 269 us
  Pallas kernels  246 us (91%)
  local copies, waits for them, and re-layouts  17.9 us (7%)
  other arithmetic  5.21 us (2%)
    pallas_call x1, Pallas kernels, mega(): pl.pallas_call(mega_kernel, in_specs=[hbm, hbm] + [vmem] * (len(ins) - 2)...  246 us
    unnamed x7, local copies, waits for them, and re-layouts  7.81 us

profile of v2, /device:TPU:1, one launch (start us, length us, event | category | flops | bytes accessed | tf_op | source)
XLA Modules:
  0.0 269.4 jit_solution(14519939860253414679)
XLA Ops:
  0.6 0.8 slice_bitcast_fusion.2
  1.5 0.8 slice_bitcast_fusion.4
  2.3 0.8 fusion
  3.1 0.8 fusion.1
  3.9 0.9 maximum_maximum_fusion
  4.8 0.5 broadcast.10
  5.3 1.3 reduce.10
  6.7 0.8 reshape.45.b1_ref
  7.5 1.3 reduce.11
  8.8 0.8 reshape.46.b2_ref
  9.7 0.7 broadcast_in_dim.4
  10.4 0.8 reshape.40.gain_ref
  11.2 0.7 broadcast_in_dim.5
  11.9 0.8 reshape.41.shift_ref
  12.8 245.6 %afno.1 = (bf16[32,2,17280]{2,1,0:T(2,128)(2,1)}, bf16[32,2,17280]{2,1,0:T(2,128)(2,1)}, f32[32,16,128]{2,1,0:T(8,128)}, f32[3,8,128]{2,1,0:T(8,128)}) custom-call(bf16[32,2,17280]{2,1,0:T(2,128)(2,1)} %tokens.1, bf16[32,2,17280]{2,1,0:T(2,128)(2,1)} %upstream.1, f32[1,17280]{1,0:T(1,128)} %reshape.40.gain_ref, f32[1,17280]{1,0:T(1,128)} %reshape.41.shift_ref, ...), custom_call_target="tpu_custom_call" | custom-call | tf_op jit(solution)/shard_map/afno/pallas_call | solution.py:475
  258.3 0.9 slice.46
  259.4 0.6 copy.34
  260.0 0.6 copy.33
  260.7 0.7 slice_bitcast_fusion
  261.4 0.8 slice_reduce_fusion
  262.2 0.6 reshape_squeeze.6
  262.8 0.6 reshape_squeeze.7
  263.4 4.6 %copy.37 = bf16[32,2,17280]{2,1,0:T(2,128)(2,1)} copy(bf16[32,2,17280]{2,1,0:T(2,128)(2,1)} %get-tuple-element.36) | data formatting | bytes 4423680
  268.0 1.4 copy.38
  (3 shorter events, 0.1 us)
Async XLA Ops:
  263.4 4.7 %copy-start = (bf16[32,2,17280]{2,1,0:T(2,128)(2,1)S(1)}, bf16[32,2,17280]{2,1,0:T(2,128)(2,1)}, u32[]{:S(2)}) copy-start(bf16[32,2,17280]{2,1,0:T(2,128)(2,1)} %get-tuple-element.37) | copy-start | bytes 6635524

commit v3 on v2

--- a/solution.py
+++ b/solution.py
@@ -72,11 +72,6 @@
     return jnp.concatenate([jnp.concatenate([re[j], im[j]], axis=0) for j in range(STEP)], axis=1)
 
 
-def big_matrix(weight):
-    real, imag = weight[0, 0], weight[1, 0]
-    return jnp.block([[real, imag], [-imag, real]])
-
-
 def lane_parts(ref_or_value):
     return [slice(c * LON, (c + 1) * LON) for c in range(GROUP)]
 
@@ -99,12 +94,13 @@
 
 
 def mega_kernel(
-    tokens, upstream, gain_ref, shift_ref, w1_ref, b1_ref, w2_ref, b2_ref,
+    gain_s, shift_s, tokens, upstream, w1_ref, b1_ref, w2_ref, b2_ref,
     lat_ref, lonh, lonl, latih, latil, lonih, lonil,
     result, grad_tokens, params_out, ends_out,
+    gain_x, shift_x, big, bias, bias_columns,
     tok, upr, cols, normed, filt, grad, spec, stash, zs, ya, yb, center, scale, first, second,
-    sums_send, sums_recv, wh, wl, wt, a1, a2, c1, c2, pack, packed_recv, piece, parts, ends_send, ends_recv,
-    load_sem, store_sem, send_sem, recv_sem, ch_send, ch_recv, small_send, small_recv,
+    sums_send, sums_recv, sums_all, wh, wl, wt, a1, a2, c1, c2, pack, packed_recv, piece, parts, ends_send, ends_recv,
+    load_sem, store_sem, send_sem, recv_sem, ch_send, ch_recv, all_send, all_recv, small_send, small_recv,
 ):
     lat = lax.axis_index("lat")
     ch = lax.axis_index("ch")
@@ -123,8 +119,8 @@
         lax.fori_loop(1, chs, lambda s, z: (fn(lax.rem(ch + s, chs)), z)[1], 0)
 
     loads = [
+        pltpu.make_async_copy(tokens, tok, load_sem.at[1]),
         pltpu.make_async_copy(upstream, upr, load_sem.at[0]),
-        pltpu.make_async_copy(tokens, tok, load_sem.at[1]),
     ]
     for c in loads:
         c.start()
@@ -132,6 +128,22 @@
     barrier = pltpu.get_barrier_semaphore()
     each_peer(lambda p: pl.semaphore_signal(barrier, inc=1, device_id={"lat": p}, device_id_type=MESH))
     each_ch(lambda p: pl.semaphore_signal(barrier, inc=1, device_id={"ch": p}, device_id_type=MESH))
+    def rows_of(ref, g):
+        return ref[:, :, lanes(g)].reshape(LAT_ROWS, SPAN).astype(f32)
+
+    def put_rows(ref, g, value):
+        ref[:, :, lanes(g)] = value.astype(bf16).reshape(32, 2, SPAN)
+
+    first[...] = jnp.zeros_like(first)
+    second[...] = jnp.zeros_like(second)
+    loads[0].wait()
+
+    @pl.loop(0, GROUPS)
+    def _(g):
+        x = rows_of(tok, g)
+        first[...] += x
+        second[...] += x * x
+
     pl.semaphore_wait(barrier, peers - 1 + chs - 1)
 
     def send_field(src, dst, kind, g):
@@ -158,26 +170,22 @@
     def keep_own(src, dst, g):
         dst[lat, :, lanes(g)] = src[lat, :, lanes(g)]
 
-    loads[0].wait()
+    loads[1].wait()
     send_field(upr, cols.at[0], UP, 0)
     send_field(upr, cols.at[0], UP, 1)
-    loads[1].wait()
-
-    def rows_of(ref, g):
-        return ref[:, :, lanes(g)].reshape(LAT_ROWS, SPAN).astype(f32)
-
-    def put_rows(ref, g, value):
-        ref[:, :, lanes(g)] = value.astype(bf16).reshape(32, 2, SPAN)
+
+    def rows8(p):
+        return pl.ds(pl.multiple_of(p * 8, 8), 8)
 
     def over_channels(which):
         sums_send[which, :, 0:LON] = narrow(first)
         sums_send[which, :, LON : 2 * LON] = narrow(second)
         sums_send[which, :, 2 * LON :] = jnp.zeros((LAT_ROWS, 384 - 2 * LON), f32)
-        sums_recv[which, ch] = sums_send[which]
+        sums_recv[which, ch] = sums_send[which, rows8(ch), :]
 
         def go(p):
             pltpu.make_async_remote_copy(
-                src_ref=sums_send.at[which],
+                src_ref=sums_send.at[which, rows8(p), :],
                 dst_ref=sums_recv.at[which, ch],
                 send_sem=ch_send.at[which],
                 recv_sem=ch_recv.at[which],
@@ -187,34 +195,59 @@
 
         each_ch(go)
 
-    def wait_channels(which):
+    def share_channels(which):
         ref = sums_recv.at[which, pl.ds(0, chs - 1)]
         pltpu.make_async_copy(ref, ref, ch_recv.at[which]).wait()
         total = sums_recv[which, 0]
         for p in range(1, chs):
             total = total + sums_recv[which, p]
-        return total * (1.0 / EMBED)
-
-    first[...] = jnp.zeros_like(first)
-    second[...] = jnp.zeros_like(second)
-
-    @pl.loop(0, GROUPS)
-    def _(g):
-        x = rows_of(tok, g)
-        first[...] += x
-        second[...] += x * x
+        sums_all[which, ch] = total * (1.0 / EMBED)
+
+        def go(p):
+            pltpu.make_async_remote_copy(
+                src_ref=sums_all.at[which, ch],
+                dst_ref=sums_all.at[which, ch],
+                send_sem=all_send.at[which],
+                recv_sem=all_recv.at[which],
+                device_id={"ch": p},
+                device_id_type=MESH,
+            ).start()
+
+        each_ch(go)
+
+    def wait_channels(which):
+        ref = sums_all.at[which, pl.ds(0, chs - 1)]
+        pltpu.make_async_copy(ref, ref, all_recv.at[which]).wait()
+        return sums_all[which].reshape(LAT_ROWS, 384)
 
     over_channels(0)
+
+    @pl.loop(0, GROUPS)
+    def _(g):
+        for source, wide in ((gain_s, gain_x), (shift_s, shift_x)):
+            for c in range(GROUP):
+                wide[g, :, c * LON : (c + 1) * LON] = jnp.full((1, LON), source[g * GROUP + c], f32)
+
+    share_channels(0)
     ya[...] = jnp.zeros_like(ya)
     yb[...] = jnp.zeros_like(yb)
-    wh[0], wl[0] = split(w1_ref[...].T)
-    wh[1], wl[1] = split(w2_ref[...].T)
-    wt[0] = w1_ref[...].astype(bf16)
-    wt[1] = w2_ref[...].astype(bf16)
+    bias[...] = jnp.zeros_like(bias)
+    for n, (w_ref, b_ref) in enumerate(((w1_ref, b1_ref), (w2_ref, b2_ref))):
+        real, imag = w_ref[0, 0], w_ref[1, 0]
+        big[:CH, :CH] = real
+        big[CH:, CH:] = real
+        big[:CH, CH:] = imag
+        big[CH:, :CH] = -imag
+        matrix = big[...]
+        wt[n] = matrix.astype(bf16)
+        wh[n], wl[n] = split(matrix.T)
+        bias[n : n + 1, 0:CH] = b_ref[0]
+        bias[n : n + 1, CH : 2 * CH] = b_ref[1]
     for g in range(GROUPS):
         keep_own(upr, cols.at[0], g)
-    for r in (a1, a2, c1, c2):
+    for r in (a1, a2, c1, c2, pack, parts):
         r[...] = jnp.zeros_like(r)
+    bias_columns[...] = bias[...].T
     sums = wait_channels(0)
     mean = sums[:, 0:LON]
     variance = sums[:, LON : 2 * LON] - mean * mean
@@ -224,7 +257,7 @@
     @pl.loop(0, GROUPS)
     def _(g):
         standard = (rows_of(tok, g) - center[...]) * scale[...]
-        put_rows(normed, g, standard * gain_ref[:, lanes(g)] + shift_ref[:, lanes(g)])
+        put_rows(normed, g, standard * gain_x[g] + shift_x[g])
         keep_own(normed, cols.at[1], g)
         send_field(normed, cols.at[1], NORM, g)
 
@@ -270,7 +303,7 @@
         at = pl.ds(i * STEP, STEP)
         re, im = spec.at[1, 0], spec.at[1, 1]
         xh, xl = split(gather_modes(re[at], im[at]))
-        pre = dot(wh[0], xh) + dot(wh[0], xl) + dot(wl[0], xh) + b1_ref[...]
+        pre = dot(wh[0], xh) + dot(wh[0], xl) + dot(wl[0], xh) + bias_columns[: 2 * CH, 0:1]
         a = math.sqrt(2.0 / math.pi)
         sq = pre * pre
         th = jnp.tanh(a * pre * (1.0 + 0.044715 * sq))
@@ -278,7 +311,7 @@
         hid = pre * half
         slope = half + 0.5 * pre * (1.0 - th * th) * (a * (1.0 + 3.0 * 0.044715 * sq))
         hh, hl = split(hid)
-        pre2 = dot(wh[1], hh) + dot(wh[1], hl) + dot(wl[1], hh) + b2_ref[...]
+        pre2 = dot(wh[1], hh) + dot(wh[1], hl) + dot(wl[1], hh) + bias_columns[: 2 * CH, 1:2]
         t = jnp.tanh(pre2 * (1.0 / shrink))
         mixed = pre2 - shrink * t
         for j in range(STEP):
@@ -339,13 +372,14 @@
         keep_own(cols.at[0], grad, g)
         send_field(cols.at[0], grad, GRAD, g)
 
-    pack[...] = jnp.zeros_like(pack)
     for n, (acc, line) in enumerate(((a1, c1), (a2, c2))):
         v = acc[...]
         top = n * 2 * CH
         pack[top : top + CH, :CH] = v[:CH, :CH] + v[CH:, CH:]
         pack[top + CH : top + 2 * CH, :CH] = v[:CH, CH:] - v[CH:, :CH]
-        pack[top : top + 2 * CH, CH : CH + 1] = jnp.sum(line[...], axis=1, keepdims=True)
+        row = jnp.sum(line[...].T, axis=0, keepdims=True)
+        pack[4 * CH + 2 * n : 4 * CH + 2 * n + 1, :CH] = row[:, :CH]
+        pack[4 * CH + 2 * n + 1 : 4 * CH + 2 * n + 2, :CH] = row[:, CH:]
 
     def rows16(p):
         return pl.ds(pl.multiple_of(p * 16, 16), 16)
@@ -370,6 +404,33 @@
         put_rows(filt, g, rows_of(tok, g) + rows_of(normed, g) + rows_of(filt, g))
         pltpu.make_async_copy(filt.at[:, :, lanes(g)], result.at[:, :, lanes(g)], store_sem.at[0, g]).start()
 
+    first[...] = jnp.zeros_like(first)
+    second[...] = jnp.zeros_like(second)
+
+    def close_part(g):
+        base = parts[:, lanes(g)]
+        column = jnp.concatenate(
+            [jnp.sum(base[:, c * LON : (c + 1) * LON], axis=1, keepdims=True) for c in range(GROUP)], axis=1
+        )
+        ends_send[g] = jnp.concatenate([column, jnp.zeros((8, 128 - GROUP), f32)], axis=1)
+
+    @pl.loop(0, GROUPS)
+    def _(g):
+        @pl.when(g > 0)
+        def _():
+            close_part(g - 1)
+
+        wait_field(grad, recv_sem, GRAD, g)
+        standard = (rows_of(tok, g) - center[...]) * scale[...]
+        total = rows_of(upr, g) + rows_of(grad, g)
+        cross = total * standard
+        gain = gain_x[g]
+        first[...] += total * gain
+        second[...] += cross * gain
+        parts[0:1, lanes(g)] = jnp.sum(cross, axis=0, keepdims=True)
+        parts[1:2, lanes(g)] = jnp.sum(total, axis=0, keepdims=True)
+
+    over_channels(1)
     wait_bytes(packed_recv, small_recv.at[0])
     piece[...] = jnp.sum(packed_recv[...], axis=0)
     params_out[lat] = piece[...]
@@ -385,33 +446,8 @@
         ).start()
 
     each_peer(send_sum)
-
-    parts[...] = jnp.zeros_like(parts)
-    first[...] = jnp.zeros_like(first)
-    second[...] = jnp.zeros_like(second)
-
-    @pl.loop(0, GROUPS)
-    def _(g):
-        wait_field(grad, recv_sem, GRAD, g)
-        standard = (rows_of(tok, g) - center[...]) * scale[...]
-        total = rows_of(upr, g) + rows_of(grad, g)
-        cross = total * standard
-        gain = gain_ref[:, lanes(g)]
-        first[...] += total * gain
-        second[...] += cross * gain
-        parts[0:1, lanes(g)] = jnp.sum(cross, axis=0, keepdims=True)
-        parts[1:2, lanes(g)] = jnp.sum(total, axis=0, keepdims=True)
-
-    over_channels(1)
-
-    @pl.loop(0, GROUPS)
-    def _(g):
-        base = parts[:, lanes(g)]
-        column = jnp.concatenate(
-            [jnp.sum(base[:, c * LON : (c + 1) * LON], axis=1, keepdims=True) for c in range(GROUP)], axis=1
-        )
-        ends_send[g] = jnp.concatenate([column, jnp.zeros((8, 128 - GROUP), f32)], axis=1)
-
+    share_channels(1)
+    close_part(GROUPS - 1)
     ends_recv[lat] = ends_send[...]
 
     def send_ends(p):
@@ -434,7 +470,7 @@
         inverse = scale[...]
         standard = (rows_of(tok, g) - center[...]) * inverse
         up = rows_of(upr, g)
-        slope = (up + rows_of(grad, g)) * gain_ref[:, lanes(g)]
+        slope = (up + rows_of(grad, g)) * gain_x[g]
         put_rows(grad, g, up + inverse * (slope - first[...] - standard * second[...]))
         pltpu.make_async_copy(grad.at[:, :, lanes(g)], grad_tokens.at[:, :, lanes(g)], store_sem.at[1, g]).start()
 
@@ -450,12 +486,62 @@
     for which in range(2):
         ref = sums_recv.at[which, pl.ds(0, chs - 1)]
         pltpu.make_async_copy(ref, ref, ch_send.at[which]).wait()
+        ref = sums_all.at[which, pl.ds(0, chs - 1)]
+        pltpu.make_async_copy(ref, ref, all_send.at[which]).wait()
     wait_bytes(packed_recv, small_send.at[0])
     wait_bytes(params_out, small_send.at[1])
     wait_bytes(ends_recv, small_send.at[2])
 
 
-def mega(tokens, upstream, gain, shift, w1, b1, w2, b2):
+PIECES = 9
+
+
+def finish_kernel(
+    result, grad_tokens, params, ends, o_result, o_grad, fw, fb, sw, sb, og, os, hold, load_sem, store_sem
+):
+    width = CH * LON // PIECES
+    pairs = ((result, o_result), (grad_tokens, o_grad))
+    at = lambda ref, i: ref.at[:, :, i * width : (i + 1) * width]
+    for i in range(PIECES):
+        for n, (src, dst) in enumerate(pairs):
+            pltpu.make_async_copy(at(src, i), at(hold.at[n], i), load_sem.at[n, i]).start()
+    p = params[...].reshape(512, 128)
+    for n, (weight, line) in enumerate(((fw, fb), (sw, sb))):
+        for part in range(2):
+            top = (2 * n + part) * CH
+            weight[part, 0] = p[top : top + CH, :CH]
+            line[part] = p[4 * CH + 2 * n + part : 4 * CH + 2 * n + part + 1, :CH]
+    for g in range(GROUPS):
+        og[:, g * GROUP : (g + 1) * GROUP] = ends[g, 0:1, :GROUP]
+        os[:, g * GROUP : (g + 1) * GROUP] = ends[g, 1:2, :GROUP]
+    for i in range(PIECES):
+        for n, (src, dst) in enumerate(pairs):
+            pltpu.make_async_copy(at(src, i), at(hold.at[n], i), load_sem.at[n, i]).wait()
+            pltpu.make_async_copy(at(hold.at[n], i), at(dst, i), store_sem.at[n, i]).start()
+    for i in range(PIECES):
+        for n, (src, dst) in enumerate(pairs):
+            pltpu.make_async_copy(at(hold.at[n], i), at(dst, i), store_sem.at[n, i]).wait()
+
+
+def finish(result, grad_tokens, params, ends):
+    hbm, vmem = pl.BlockSpec(memory_space=pl.ANY), pl.BlockSpec(memory_space=pltpu.VMEM)
+    field = jax.ShapeDtypeStruct((32, 2, CH * LON), bf16)
+    weight, line, vec = [jax.ShapeDtypeStruct(x, f32) for x in ((2, 1, CH, CH), (2, 1, CH), (1, CH))]
+    return pl.pallas_call(
+        finish_kernel,
+        in_specs=[hbm, hbm, vmem, vmem],
+        out_specs=[hbm, hbm] + [vmem] * 6,
+        out_shape=[field, field, weight, line, weight, line, vec, vec],
+        scratch_shapes=[
+            pltpu.VMEM((2, 32, 2, CH * LON), bf16),
+            pltpu.SemaphoreType.DMA((2, PIECES)), pltpu.SemaphoreType.DMA((2, PIECES)),
+        ],
+        compiler_params=pltpu.CompilerParams(vmem_limit_bytes=67_043_328),
+        name="finish",
+    )(result, grad_tokens, params, ends)
+
+
+def mega(gain, shift, tokens, upstream, w1, b1, w2, b2):
     lat, lon, lon2 = tables()
     pair = lambda a, b: [jnp.asarray(np.stack(x)) for x in zip(split_table(a), split_table(b))]
     lat_h, lat_l = split_table(lat)
@@ -463,18 +549,19 @@
     lonh, lonl = pair(lon2, lon)
     lonih, lonil = pair(lon.T, lon2.T)
     hbm, vmem = pl.BlockSpec(memory_space=pl.ANY), pl.BlockSpec(memory_space=pltpu.VMEM)
+    smem = pl.BlockSpec(memory_space=pltpu.SMEM)
     field = jax.ShapeDtypeStruct((32, 2, CH * LON), bf16)
     V, D = pltpu.VMEM, pltpu.SemaphoreType.DMA
     fld = V((32, 2, CH * LON), bf16)
     wide = V((LAT_ROWS, SPAN), f32)
     ins = [
-        tokens, upstream, gain, shift, w1, b1, w2, b2,
+        gain, shift, tokens, upstream, w1, b1, w2, b2,
         jnp.asarray(np.concatenate([lat_h, lat_l], axis=0)), lonh, lonl,
         jnp.asarray(lati_h), jnp.asarray(lati_l), lonih, lonil,
     ]
     return pl.pallas_call(
         mega_kernel,
-        in_specs=[hbm, hbm] + [vmem] * (len(ins) - 2),
+        in_specs=[smem, smem, hbm, hbm] + [vmem] * (len(ins) - 4),
         out_specs=[hbm, hbm, vmem, vmem],
         out_shape=[
             field, field,
@@ -482,17 +569,18 @@
             jax.ShapeDtypeStruct((GROUPS, 8, 128), f32),
         ],
         scratch_shapes=[
+            V((GROUPS, 1, SPAN), f32), V((GROUPS, 1, SPAN), f32), V((192, 192), f32), V((8, 256), f32), V((256, 8), f32),
             fld, fld, V((2, 32, 2, CH * LON), bf16), fld, fld, fld,
             V((2, 2, LAT_ROWS, CH, 128), f32),
             V((4, LAT_ROWS // STEP, 2 * CH, 128 * STEP), bf16),
             wide, V((LAT_ROWS * PITCH, 128), f32), V((LAT_ROWS * PITCH, 128), f32),
             wide, wide, wide, wide,
-            V((2, LAT_ROWS, 384), f32), V((2, 8, LAT_ROWS, 384), f32),
+            V((2, LAT_ROWS, 384), f32), V((2, 8, 8, 384), f32), V((2, 8, 8, 384), f32),
             V((2, 192, 192), bf16), V((2, 192, 192), bf16), V((2, 192, 192), bf16),
             V((192, 192), f32), V((192, 192), f32), V((192, 128), f32), V((192, 128), f32),
             V((512, 128), f32), V((32, 16, 128), f32), V((16, 128), f32),
             V((8, CH * LON), f32), V((GROUPS, 8, 128), f32), V((32, GROUPS, 8, 128), f32),
-            D((2,)), D((2, GROUPS)), D((4, GROUPS)), D((4, GROUPS)), D((2,)), D((2,)), D((3,)), D((3,)),
+            D((2,)), D((2, GROUPS)), D((4, GROUPS)), D((4, GROUPS)), D((2,)), D((2,)), D((2,)), D((2,)), D((3,)), D((3,)),
         ],
         compiler_params=pltpu.CompilerParams(
             collective_id=0, has_side_effects=True, vmem_limit_bytes=67_043_328
@@ -504,18 +592,11 @@
 def body(
     tokens, norm_gain, norm_shift, first_weight, first_bias, second_weight, second_bias, upstream
 ):
-    wide = lambda v: jnp.broadcast_to(v[:, None], (CH, LON)).reshape(1, CH * LON)
-    result, grad_tokens, params, ends = mega(
-        tokens, upstream, wide(norm_gain), wide(norm_shift),
-        big_matrix(first_weight), first_bias.reshape(2 * CH, 1),
-        big_matrix(second_weight), second_bias.reshape(2 * CH, 1),
+    ends = mega(
+        norm_gain, norm_shift, tokens, upstream, first_weight, first_bias, second_weight, second_bias
     )
-    params = params.reshape(512, 128)[: 4 * CH].reshape(2, 2, 1, CH, 128)
-    weights, biases = params[..., :CH], params[..., CH]
-    return (
-        result, grad_tokens, weights[0], biases[0], weights[1], biases[1],
-        ends[:, 0, :GROUP].reshape(CH), ends[:, 1, :GROUP].reshape(CH),
-    )
+    result, grad_tokens, fw, fb, sw, sb, gain, shift = finish(*ends)
+    return result, grad_tokens, fw, fb, sw, sb, gain.reshape(CH), shift.reshape(CH)
 
 
 def solution(mesh):

time: 270 us -> 242 us (0.90)
  local copies, waits for them, and re-layouts: 17.9 us -> 0 us
  other arithmetic: 5.21 us -> 0 us
  Pallas kernels: 246 us -> 241 us
    unnamed x7 -> x0, local copies, waits for them, and re-layouts: 7.81 us -> none
    pallas_call x1 -> x2, Pallas kernels: 246 us -> 241 us  [the longest x1 235 us: mega(): pl.pallas_call(mega_kernel, in_specs=[smem, smem, hbm, hbm] + [vmem] * (l...]
    reshape x4 -> x0, local copies, waits for them, and re-layouts: 3.27 us -> none  [the longest x2 1.64 us: body(): jnp.broadcast_to(v[:, None], (CH, LON)).reshape(1, CH * LON)]
where the time goes in v3:
time: 242 us
  Pallas kernels  241 us (100%)
    pallas_call x1, Pallas kernels, mega(): pl.pallas_call(mega_kernel, in_specs=[smem, smem, hbm, hbm] + [vmem] * (l...  235 us
    pallas_call x1, Pallas kernels, finish(): pl.pallas_call(finish_kernel, in_specs=[hbm, hbm, vmem, vmem], out_specs=...  6.18 us

profile of v3, /device:TPU:1, one launch (start us, length us, event | category | flops | bytes accessed | tf_op | source)
XLA Modules:
  0.0 241.6 jit_solution(10697525612805680770)
XLA Ops:
  0.6 234.6 %afno.1 = (bf16[32,2,17280]{2,1,0:T(2,128)(2,1)}, bf16[32,2,17280]{2,1,0:T(2,128)(2,1)}, f32[32,16,128]{2,1,0:T(8,128)}, f32[3,8,128]{2,1,0:T(8,128)}) custom-call(f32[96]{0:T(128)} %gain_s.1, f32[96]{0:T(128)} %shift_s.1, bf16[32,2,17280]{2,1,0:T(2,128)(2,1)} %tokens.1, bf16[32,2,17280]{2,1,0:T(2,128)(2,1)} %upstream.1, f32[2,1,96,96]{3,2,1,0:T(8,128)} %w1_ref.1, ...), custom_call_target="tpu_custom_call" | custom-call | tf_op jit(solution)/shard_map/afno/pallas_call | solution.py:562
  235.2 6.2 %finish.1 = (bf16[32,2,17280]{2,1,0:T(2,128)(2,1)}, bf16[32,2,17280]{2,1,0:T(2,128)(2,1)}, f32[2,1,96,96]{3,2,1,0:T(8,128)}, f32[2,1,96]{2,1,0:T(1,128)}, f32[2,...) custom-call(bf16[32,2,17280]{2,1,0:T(2,128)(2,1)} %get-tuple-element.20.result, ...), custom_call_target="tpu_custom_call" | custom-call | tf_op jit(solution)/shard_map/finish/pallas_call | solution.py:530

commit v4 on v3

--- a/solution.py
+++ b/solution.py
@@ -94,12 +94,13 @@
 
 
 def mega_kernel(
-    gain_s, shift_s, tokens, upstream, w1_ref, b1_ref, w2_ref, b2_ref,
-    lat_ref, lonh, lonl, latih, latil, lonih, lonil,
+    gain_s, shift_s, tokens, upstream, w1_hbm, b1_hbm, w2_hbm, b2_hbm,
+    lat_hbm, lonh_hbm, lonl_hbm, latih_hbm, latil_hbm, lonih_hbm, lonil_hbm,
     result, grad_tokens, params_out, ends_out,
+    w1_ref, b1_ref, w2_ref, b2_ref, lat_ref, lonh, lonl, latih, latil, lonih, lonil, table_sem,
     gain_x, shift_x, big, bias, bias_columns,
-    tok, upr, cols, normed, filt, grad, spec, stash, zs, ya, yb, center, scale, first, second,
-    sums_send, sums_recv, sums_all, wh, wl, wt, a1, a2, c1, c2, pack, packed_recv, piece, parts, ends_send, ends_recv,
+    tok, upr, cols, away, normed, filt, grad, spec, stash, zs, ya, yb, center, scale, first, second,
+    sums_send, sums_recv, sums_all, wh, wl, wt, a1, a2, c1, c2, pack, pack16, packed_recv, piece, parts, ends_send, ends_recv, mean_send, mean_recv,
     load_sem, store_sem, send_sem, recv_sem, ch_send, ch_recv, all_send, all_recv, small_send, small_recv,
 ):
     lat = lax.axis_index("lat")
@@ -118,33 +119,32 @@
     def each_ch(fn):
         lax.fori_loop(1, chs, lambda s, z: (fn(lax.rem(ch + s, chs)), z)[1], 0)
 
+    barrier = pltpu.get_barrier_semaphore()
+    each_peer(lambda p: pl.semaphore_signal(barrier, inc=1, device_id={"lat": p}, device_id_type=MESH))
+    each_ch(lambda p: pl.semaphore_signal(barrier, inc=1, device_id={"ch": p}, device_id_type=MESH))
     loads = [
+        pltpu.make_async_copy(upstream, upr, load_sem.at[0]),
         pltpu.make_async_copy(tokens, tok, load_sem.at[1]),
-        pltpu.make_async_copy(upstream, upr, load_sem.at[0]),
     ]
     for c in loads:
         c.start()
 
-    barrier = pltpu.get_barrier_semaphore()
-    each_peer(lambda p: pl.semaphore_signal(barrier, inc=1, device_id={"lat": p}, device_id_type=MESH))
-    each_ch(lambda p: pl.semaphore_signal(barrier, inc=1, device_id={"ch": p}, device_id_type=MESH))
+    sources = (
+        (w1_hbm, w1_ref), (b1_hbm, b1_ref), (w2_hbm, w2_ref), (b2_hbm, b2_ref), (lat_hbm, lat_ref),
+        (lonh_hbm, lonh), (lonl_hbm, lonl), (latih_hbm, latih), (latil_hbm, latil),
+        (lonih_hbm, lonih), (lonil_hbm, lonil),
+    )
+    table_loads = [pltpu.make_async_copy(src, dst, table_sem.at[n]) for n, (src, dst) in enumerate(sources)]
+    for c in table_loads:
+        c.start()
+
+    pl.semaphore_wait(barrier, peers - 1 + chs - 1)
+
     def rows_of(ref, g):
         return ref[:, :, lanes(g)].reshape(LAT_ROWS, SPAN).astype(f32)
 
     def put_rows(ref, g, value):
         ref[:, :, lanes(g)] = value.astype(bf16).reshape(32, 2, SPAN)
-
-    first[...] = jnp.zeros_like(first)
-    second[...] = jnp.zeros_like(second)
-    loads[0].wait()
-
-    @pl.loop(0, GROUPS)
-    def _(g):
-        x = rows_of(tok, g)
-        first[...] += x
-        second[...] += x * x
-
-    pl.semaphore_wait(barrier, peers - 1 + chs - 1)
 
     def send_field(src, dst, kind, g):
         def go(p):
@@ -170,9 +170,18 @@
     def keep_own(src, dst, g):
         dst[lat, :, lanes(g)] = src[lat, :, lanes(g)]
 
-    loads[1].wait()
+    loads[0].wait()
     send_field(upr, cols.at[0], UP, 0)
     send_field(upr, cols.at[0], UP, 1)
+    first[...] = jnp.zeros_like(first)
+    second[...] = jnp.zeros_like(second)
+    loads[1].wait()
+
+    @pl.loop(0, GROUPS)
+    def _(g):
+        x = rows_of(tok, g)
+        first[...] += x
+        second[...] += x * x
 
     def rows8(p):
         return pl.ds(pl.multiple_of(p * 8, 8), 8)
@@ -229,6 +238,8 @@
                 wide[g, :, c * LON : (c + 1) * LON] = jnp.full((1, LON), source[g * GROUP + c], f32)
 
     share_channels(0)
+    for c in table_loads:
+        c.wait()
     ya[...] = jnp.zeros_like(ya)
     yb[...] = jnp.zeros_like(yb)
     bias[...] = jnp.zeros_like(bias)
@@ -322,7 +333,7 @@
         stash[2, i] = hh
         stash[3, i] = (t * t).astype(bf16)
 
-    def field_of(field, g, dst):
+    def field_of(field, g):
         here = pl.ds(pl.multiple_of(g * GROUP, GROUP), GROUP)
         gr, gi = spec[field, 0, :, here], spec[field, 1, :, here]
         left = jnp.concatenate([gr[0:1], gr[1:32] + gr[33:64], gr[32:33], gi[33:64] - gi[1:32]], axis=0)
@@ -337,13 +348,13 @@
             zs[:, c * LON : c * LON + 128] = ya[pl.ds(c, LAT_ROWS, stride=PITCH), :]
             zs[:, c * LON + 128 : (c + 1) * LON] = yb[pl.ds(c, LAT_ROWS, stride=PITCH), 0 : LON - 128]
         z = zs[...].astype(bf16)
-        put_rows(dst, g, dot(latih[...], z) + dot(latil[...], z))
-
-    @pl.loop(0, GROUPS)
-    def _(g):
-        field_of(1, g, cols.at[1])
-        keep_own(cols.at[1], filt, g)
-        send_field(cols.at[1], filt, FILT, g)
+        return dot(latih[...], z) + dot(latil[...], z)
+
+    @pl.loop(0, GROUPS)
+    def _(g):
+        put_rows(away, g, field_of(1, g))
+        keep_own(away, filt, g)
+        send_field(away, filt, FILT, g)
 
     wait_field(cols.at[0], recv_sem, UP, 2)
     yb[:, LON - 128 :] = jnp.zeros((LAT_ROWS * PITCH, 256 - LON), f32)
@@ -366,12 +377,6 @@
         c2[...] += sum(p2[:, 128 * j : 128 * (j + 1)] for j in range(STEP))
         c1[...] += sum(p1[:, 128 * j : 128 * (j + 1)] for j in range(STEP))
 
-    @pl.loop(0, GROUPS)
-    def _(g):
-        field_of(0, g, cols.at[0])
-        keep_own(cols.at[0], grad, g)
-        send_field(cols.at[0], grad, GRAD, g)
-
     for n, (acc, line) in enumerate(((a1, c1), (a2, c2))):
         v = acc[...]
         top = n * 2 * CH
@@ -381,14 +386,16 @@
         pack[4 * CH + 2 * n : 4 * CH + 2 * n + 1, :CH] = row[:, :CH]
         pack[4 * CH + 2 * n + 1 : 4 * CH + 2 * n + 2, :CH] = row[:, CH:]
 
+    pack16[...] = pack[...].astype(bf16)
+
     def rows16(p):
         return pl.ds(pl.multiple_of(p * 16, 16), 16)
 
-    packed_recv[lat] = pack[rows16(lat), :]
+    packed_recv[lat] = pack16[rows16(lat), :]
 
     def send_piece(p):
         pltpu.make_async_remote_copy(
-            src_ref=pack.at[rows16(p), :],
+            src_ref=pack16.at[rows16(p), :],
             dst_ref=packed_recv.at[lat],
             send_sem=small_send.at[0],
             recv_sem=small_recv.at[0],
@@ -398,41 +405,48 @@
 
     each_peer(send_piece)
 
+    first[...] = jnp.zeros_like(first)
+    second[...] = jnp.zeros_like(second)
+
+    @pl.loop(0, GROUPS)
+    def _(g):
+        out = field_of(0, g).astype(bf16)
+        total = rows_of(cols.at[0], g) + out.astype(f32)
+        first[...] += total * gain_x[g]
+        second[...] += total * (rows_of(cols.at[1], g) - shift_x[g])
+        put_rows(cols.at[0], g, out)
+        keep_own(cols.at[0], grad, g)
+
+        @pl.when(g < GROUPS - 1)
+        def _():
+            send_field(cols.at[0], grad, GRAD, g)
+
+    over_channels(1)
+    share_channels(1)
+    mean_send[...] = wait_channels(1).reshape(32, 2, 384)
+    mean_recv[lat] = mean_send[lat]
+
+    def send_mean(p):
+        pltpu.make_async_remote_copy(
+            src_ref=mean_send.at[p],
+            dst_ref=mean_recv.at[lat],
+            send_sem=small_send.at[3],
+            recv_sem=small_recv.at[3],
+            device_id={"lat": p},
+            device_id_type=MESH,
+        ).start()
+
+    each_peer(send_mean)
+    send_field(cols.at[0], grad, GRAD, GROUPS - 1)
+
     @pl.loop(0, GROUPS)
     def _(g):
         wait_field(filt, recv_sem, FILT, g)
         put_rows(filt, g, rows_of(tok, g) + rows_of(normed, g) + rows_of(filt, g))
         pltpu.make_async_copy(filt.at[:, :, lanes(g)], result.at[:, :, lanes(g)], store_sem.at[0, g]).start()
 
-    first[...] = jnp.zeros_like(first)
-    second[...] = jnp.zeros_like(second)
-
-    def close_part(g):
-        base = parts[:, lanes(g)]
-        column = jnp.concatenate(
-            [jnp.sum(base[:, c * LON : (c + 1) * LON], axis=1, keepdims=True) for c in range(GROUP)], axis=1
-        )
-        ends_send[g] = jnp.concatenate([column, jnp.zeros((8, 128 - GROUP), f32)], axis=1)
-
-    @pl.loop(0, GROUPS)
-    def _(g):
-        @pl.when(g > 0)
-        def _():
-            close_part(g - 1)
-
-        wait_field(grad, recv_sem, GRAD, g)
-        standard = (rows_of(tok, g) - center[...]) * scale[...]
-        total = rows_of(upr, g) + rows_of(grad, g)
-        cross = total * standard
-        gain = gain_x[g]
-        first[...] += total * gain
-        second[...] += cross * gain
-        parts[0:1, lanes(g)] = jnp.sum(cross, axis=0, keepdims=True)
-        parts[1:2, lanes(g)] = jnp.sum(total, axis=0, keepdims=True)
-
-    over_channels(1)
     wait_bytes(packed_recv, small_recv.at[0])
-    piece[...] = jnp.sum(packed_recv[...], axis=0)
+    piece[...] = jnp.sum(packed_recv[...].astype(f32), axis=0).astype(bf16)
     params_out[lat] = piece[...]
 
     def send_sum(p):
@@ -446,7 +460,36 @@
         ).start()
 
     each_peer(send_sum)
-    share_channels(1)
+
+    wait_bytes(mean_recv, small_recv.at[3])
+    means = mean_recv[...].reshape(LAT_ROWS, 384)
+    widen(first, means[:, 0:LON])
+    widen(second, means[:, LON : 2 * LON])
+
+    def close_part(g):
+        base = parts[:, g * SPAN : (g + 1) * SPAN]
+        column = jnp.concatenate(
+            [jnp.sum(base[:, c * LON : (c + 1) * LON], axis=1, keepdims=True) for c in range(GROUP)], axis=1
+        )
+        ends_send[:, g * GROUP : (g + 1) * GROUP] = column[0:2]
+
+    ends_send[...] = jnp.zeros_like(ends_send)
+
+    @pl.loop(0, GROUPS)
+    def _(g):
+        for k in range(GROUPS - 1):
+            pl.when(g == k + 1)(functools.partial(close_part, k))
+        wait_field(grad, recv_sem, GRAD, g)
+        inverse = scale[...]
+        standard = (rows_of(tok, g) - center[...]) * inverse
+        up = rows_of(upr, g)
+        total = up + rows_of(grad, g)
+        parts[0:1, lanes(g)] = jnp.sum(total * standard, axis=0, keepdims=True)
+        parts[1:2, lanes(g)] = jnp.sum(total, axis=0, keepdims=True)
+        slope = total * gain_x[g]
+        put_rows(grad, g, up + inverse * (slope - first[...] - standard * second[...]))
+        pltpu.make_async_copy(grad.at[:, :, lanes(g)], grad_tokens.at[:, :, lanes(g)], store_sem.at[1, g]).start()
+
     close_part(GROUPS - 1)
     ends_recv[lat] = ends_send[...]
 
@@ -461,26 +504,13 @@
         ).start()
 
     each_peer(send_ends)
-    sums = wait_channels(1)
-    widen(first, sums[:, 0:LON])
-    widen(second, sums[:, LON : 2 * LON])
-
-    @pl.loop(0, GROUPS)
-    def _(g):
-        inverse = scale[...]
-        standard = (rows_of(tok, g) - center[...]) * inverse
-        up = rows_of(upr, g)
-        slope = (up + rows_of(grad, g)) * gain_x[g]
-        put_rows(grad, g, up + inverse * (slope - first[...] - standard * second[...]))
-        pltpu.make_async_copy(grad.at[:, :, lanes(g)], grad_tokens.at[:, :, lanes(g)], store_sem.at[1, g]).start()
-
     wait_bytes(ends_recv, small_recv.at[2])
     ends_out[...] = jnp.sum(ends_recv[...], axis=0)
     wait_bytes(params_out, small_recv.at[1])
     for which, buf, out in ((0, filt, result), (1, grad, grad_tokens)):
         for g in range(GROUPS):
             pltpu.make_async_copy(buf.at[:, :, lanes(g)], out.at[:, :, lanes(g)], store_sem.at[which, g]).wait()
-    for kind, buf in ((UP, upr), (NORM, normed), (FILT, cols.at[1]), (GRAD, cols.at[0])):
+    for kind, buf in ((UP, upr), (NORM, normed), (FILT, away), (GRAD, cols.at[0])):
         for g in range(GROUPS):
             wait_field(buf, send_sem, kind, g)
     for which in range(2):
@@ -491,50 +521,70 @@
     wait_bytes(packed_recv, small_send.at[0])
     wait_bytes(params_out, small_send.at[1])
     wait_bytes(ends_recv, small_send.at[2])
+    wait_bytes(mean_recv, small_send.at[3])
 
 
 PIECES = 9
 
 
 def finish_kernel(
-    result, grad_tokens, params, ends, o_result, o_grad, fw, fb, sw, sb, og, os, hold, load_sem, store_sem
+    result, grad_tokens, params, ends, o_result, o_grad, o_fw, o_fb, o_sw, o_sb, o_og, o_os,
+    hold, params_v, ends_v, fw, fb, sw, sb, og, os, load_sem, store_sem, small_load, small_store,
 ):
     width = CH * LON // PIECES
     pairs = ((result, o_result), (grad_tokens, o_grad))
     at = lambda ref, i: ref.at[:, :, i * width : (i + 1) * width]
-    for i in range(PIECES):
-        for n, (src, dst) in enumerate(pairs):
-            pltpu.make_async_copy(at(src, i), at(hold.at[n], i), load_sem.at[n, i]).start()
-    p = params[...].reshape(512, 128)
+    small = [
+        pltpu.make_async_copy(params, params_v, small_load.at[0]),
+        pltpu.make_async_copy(ends, ends_v, small_load.at[1]),
+    ]
+    loads = [
+        [pltpu.make_async_copy(at(src, i), at(hold.at[n], i), load_sem.at[n, i]) for n, (src, _) in enumerate(pairs)]
+        for i in range(PIECES)
+    ]
+    stores = [
+        [pltpu.make_async_copy(at(hold.at[n], i), at(dst, i), store_sem.at[n, i]) for n, (_, dst) in enumerate(pairs)]
+        for i in range(PIECES)
+    ]
+    for c in small + sum(loads, []):
+        c.start()
+    for c in small:
+        c.wait()
+    p = params_v[...].astype(f32).reshape(512, 128)
     for n, (weight, line) in enumerate(((fw, fb), (sw, sb))):
         for part in range(2):
             top = (2 * n + part) * CH
             weight[part, 0] = p[top : top + CH, :CH]
             line[part] = p[4 * CH + 2 * n + part : 4 * CH + 2 * n + part + 1, :CH]
-    for g in range(GROUPS):
-        og[:, g * GROUP : (g + 1) * GROUP] = ends[g, 0:1, :GROUP]
-        os[:, g * GROUP : (g + 1) * GROUP] = ends[g, 1:2, :GROUP]
+    og[...] = ends_v[0:1, :CH]
+    os[...] = ends_v[1:2, :CH]
+    outs = ((fw, o_fw), (fb, o_fb), (sw, o_sw), (sb, o_sb), (og, o_og), (os, o_os))
+    small = [pltpu.make_async_copy(src, dst, small_store.at[n]) for n, (src, dst) in enumerate(outs)]
+    for c in small:
+        c.start()
     for i in range(PIECES):
-        for n, (src, dst) in enumerate(pairs):
-            pltpu.make_async_copy(at(src, i), at(hold.at[n], i), load_sem.at[n, i]).wait()
-            pltpu.make_async_copy(at(hold.at[n], i), at(dst, i), store_sem.at[n, i]).start()
-    for i in range(PIECES):
-        for n, (src, dst) in enumerate(pairs):
-            pltpu.make_async_copy(at(hold.at[n], i), at(dst, i), store_sem.at[n, i]).wait()
+        for n in range(2):
+            loads[i][n].wait()
+            stores[i][n].start()
+    for c in small + sum(stores, []):
+        c.wait()
 
 
 def finish(result, grad_tokens, params, ends):
-    hbm, vmem = pl.BlockSpec(memory_space=pl.ANY), pl.BlockSpec(memory_space=pltpu.VMEM)
+    hbm = pl.BlockSpec(memory_space=pl.ANY)
     field = jax.ShapeDtypeStruct((32, 2, CH * LON), bf16)
     weight, line, vec = [jax.ShapeDtypeStruct(x, f32) for x in ((2, 1, CH, CH), (2, 1, CH), (1, CH))]
+    small = [weight, line, weight, line, vec, vec]
     return pl.pallas_call(
         finish_kernel,
-        in_specs=[hbm, hbm, vmem, vmem],
-        out_specs=[hbm, hbm] + [vmem] * 6,
-        out_shape=[field, field, weight, line, weight, line, vec, vec],
+        in_specs=[hbm] * 4,
+        out_specs=[hbm] * 8,
+        out_shape=[field, field] + small,
         scratch_shapes=[
             pltpu.VMEM((2, 32, 2, CH * LON), bf16),
+            *[pltpu.VMEM(x.shape, x.dtype) for x in (params, ends, *small)],
             pltpu.SemaphoreType.DMA((2, PIECES)), pltpu.SemaphoreType.DMA((2, PIECES)),
+            pltpu.SemaphoreType.DMA((2,)), pltpu.SemaphoreType.DMA((6,)),
         ],
         compiler_params=pltpu.CompilerParams(vmem_limit_bytes=67_043_328),
         name="finish",
@@ -561,16 +611,17 @@
     ]
     return pl.pallas_call(
         mega_kernel,
-        in_specs=[smem, smem, hbm, hbm] + [vmem] * (len(ins) - 4),
+        in_specs=[smem, smem] + [hbm] * (len(ins) - 2),
         out_specs=[hbm, hbm, vmem, vmem],
         out_shape=[
             field, field,
-            jax.ShapeDtypeStruct((32, 16, 128), f32),
-            jax.ShapeDtypeStruct((GROUPS, 8, 128), f32),
+            jax.ShapeDtypeStruct((32, 16, 128), bf16),
+            jax.ShapeDtypeStruct((2, 128), f32),
         ],
         scratch_shapes=[
+            *[V(x.shape, x.dtype) for x in ins[4:]], D((len(ins) - 4,)),
             V((GROUPS, 1, SPAN), f32), V((GROUPS, 1, SPAN), f32), V((192, 192), f32), V((8, 256), f32), V((256, 8), f32),
-            fld, fld, V((2, 32, 2, CH * LON), bf16), fld, fld, fld,
+            fld, fld, V((2, 32, 2, CH * LON), bf16), fld, fld, fld, fld,
             V((2, 2, LAT_ROWS, CH, 128), f32),
             V((4, LAT_ROWS // STEP, 2 * CH, 128 * STEP), bf16),
             wide, V((LAT_ROWS * PITCH, 128), f32), V((LAT_ROWS * PITCH, 128), f32),
@@ -578,9 +629,9 @@
             V((2, LAT_ROWS, 384), f32), V((2, 8, 8, 384), f32), V((2, 8, 8, 384), f32),
             V((2, 192, 192), bf16), V((2, 192, 192), bf16), V((2, 192, 192), bf16),
             V((192, 192), f32), V((192, 192), f32), V((192, 128), f32), V((192, 128), f32),
-            V((512, 128), f32), V((32, 16, 128), f32), V((16, 128), f32),
-            V((8, CH * LON), f32), V((GROUPS, 8, 128), f32), V((32, GROUPS, 8, 128), f32),
-            D((2,)), D((2, GROUPS)), D((4, GROUPS)), D((4, GROUPS)), D((2,)), D((2,)), D((2,)), D((2,)), D((3,)), D((3,)),
+            V((512, 128), f32), V((512, 128), bf16), V((32, 16, 128), bf16), V((16, 128), bf16),
+            V((8, CH * LON), f32), V((2, 128), f32), V((32, 2, 128), f32), V((32, 2, 384), f32), V((32, 2, 384), f32),
+            D((2,)), D((2, GROUPS)), D((4, GROUPS)), D((4, GROUPS)), D((2,)), D((2,)), D((2,)), D((2,)), D((4,)), D((4,)),
         ],
         compiler_params=pltpu.CompilerParams(
             collective_id=0, has_side_effects=True, vmem_limit_bytes=67_043_328

time: 242 us -> 232 us (0.959)
  Pallas kernels: 241 us -> 231 us
    pallas_call x2, Pallas kernels: 241 us -> 231 us  [the longest x1 226 us: mega(): pl.pallas_call(mega_kernel, in_specs=[smem, smem] + [hbm] * (len(ins) - 2...]
where the time goes in v4:
time: 232 us
  Pallas kernels  231 us (100%)
    pallas_call x1, Pallas kernels, mega(): pl.pallas_call(mega_kernel, in_specs=[smem, smem] + [hbm] * (len(ins) - 2...  226 us
    pallas_call x1, Pallas kernels, finish(): pl.pallas_call(finish_kernel, in_specs=[hbm] * 4, out_specs=[hbm] * 8, ou...  4.81 us

profile of v4, /device:TPU:1, one launch (start us, length us, event | category | flops | bytes accessed | tf_op | source)
XLA Modules:
  0.0 232.0 jit_solution(16273610444589175958)
XLA Ops:
  0.6 226.4 %afno.1 = (bf16[32,2,17280]{2,1,0:T(2,128)(2,1)}, bf16[32,2,17280]{2,1,0:T(2,128)(2,1)}, bf16[32,16,128]{2,1,0:T(8,128)(2,1)}, f32[2,128]{1,0:T(2,128)}) custom-call(f32[96]{0:T(128)} %gain_s.1, f32[96]{0:T(128)} %shift_s.1, bf16[32,2,17280]{2,1,0:T(2,128)(2,1)} %tokens.1, bf16[32,2,17280]{2,1,0:T(2,128)(2,1)} %upstream.1, f32[2,1,96,96]{3,2,1,0:T(8,128)} %w1_hbm.1, ...), custom_call_target="tpu_custom_call" | custom-call | tf_op jit(solution)/shard_map/afno/pallas_call | solution.py:612
  227.1 4.8 %finish.1 = (bf16[32,2,17280]{2,1,0:T(2,128)(2,1)}, bf16[32,2,17280]{2,1,0:T(2,128)(2,1)}, f32[2,1,96,96]{3,2,1,0:T(8,128)}, f32[2,1,96]{2,1,0:T(1,128)}, f32[2,...) custom-call(bf16[32,2,17280]{2,1,0:T(2,128)(2,1)} %get-tuple-element.20.result, ...), custom_call_target="tpu_custom_call" | custom-call | tf_op jit(solution)/shard_map/finish/pallas_call | solution.py:578

commit v5 on v4

--- a/solution.py
+++ b/solution.py
@@ -94,10 +94,10 @@
 
 
 def mega_kernel(
-    gain_s, shift_s, tokens, upstream, w1_hbm, b1_hbm, w2_hbm, b2_hbm,
+    gain_hbm, shift_hbm, tokens, upstream, w1_hbm, b1_hbm, w2_hbm, b2_hbm,
     lat_hbm, lonh_hbm, lonl_hbm, latih_hbm, latil_hbm, lonih_hbm, lonil_hbm,
     result, grad_tokens, params_out, ends_out,
-    w1_ref, b1_ref, w2_ref, b2_ref, lat_ref, lonh, lonl, latih, latil, lonih, lonil, table_sem,
+    w1_ref, b1_ref, w2_ref, b2_ref, lat_ref, lonh, lonl, latih, latil, lonih, lonil, gain_s, shift_s, table_sem,
     gain_x, shift_x, big, bias, bias_columns,
     tok, upr, cols, away, normed, filt, grad, spec, stash, zs, ya, yb, center, scale, first, second,
     sums_send, sums_recv, sums_all, wh, wl, wt, a1, a2, c1, c2, pack, pack16, packed_recv, piece, parts, ends_send, ends_recv, mean_send, mean_recv,
@@ -132,7 +132,7 @@
     sources = (
         (w1_hbm, w1_ref), (b1_hbm, b1_ref), (w2_hbm, w2_ref), (b2_hbm, b2_ref), (lat_hbm, lat_ref),
         (lonh_hbm, lonh), (lonl_hbm, lonl), (latih_hbm, latih), (latil_hbm, latil),
-        (lonih_hbm, lonih), (lonil_hbm, lonil),
+        (lonih_hbm, lonih), (lonil_hbm, lonil), (gain_hbm, gain_s), (shift_hbm, shift_s),
     )
     table_loads = [pltpu.make_async_copy(src, dst, table_sem.at[n]) for n, (src, dst) in enumerate(sources)]
     for c in table_loads:
@@ -230,6 +230,8 @@
         return sums_all[which].reshape(LAT_ROWS, 384)
 
     over_channels(0)
+    for c in table_loads:
+        c.wait()
 
     @pl.loop(0, GROUPS)
     def _(g):
@@ -238,8 +240,6 @@
                 wide[g, :, c * LON : (c + 1) * LON] = jnp.full((1, LON), source[g * GROUP + c], f32)
 
     share_channels(0)
-    for c in table_loads:
-        c.wait()
     ya[...] = jnp.zeros_like(ya)
     yb[...] = jnp.zeros_like(yb)
     bias[...] = jnp.zeros_like(bias)
@@ -475,23 +475,19 @@
 
     ends_send[...] = jnp.zeros_like(ends_send)
 
-    @pl.loop(0, GROUPS)
-    def _(g):
-        for k in range(GROUPS - 1):
-            pl.when(g == k + 1)(functools.partial(close_part, k))
-        wait_field(grad, recv_sem, GRAD, g)
+    def sum_part(g):
+        standard = (rows_of(tok, g) - center[...]) * scale[...]
+        total = rows_of(upr, g) + rows_of(grad, g)
+        parts[0:1, lanes(g)] = jnp.sum(total * standard, axis=0, keepdims=True)
+        parts[1:2, lanes(g)] = jnp.sum(total, axis=0, keepdims=True)
+
+    def finish_tokens(g):
         inverse = scale[...]
         standard = (rows_of(tok, g) - center[...]) * inverse
         up = rows_of(upr, g)
-        total = up + rows_of(grad, g)
-        parts[0:1, lanes(g)] = jnp.sum(total * standard, axis=0, keepdims=True)
-        parts[1:2, lanes(g)] = jnp.sum(total, axis=0, keepdims=True)
-        slope = total * gain_x[g]
+        slope = (up + rows_of(grad, g)) * gain_x[g]
         put_rows(grad, g, up + inverse * (slope - first[...] - standard * second[...]))
         pltpu.make_async_copy(grad.at[:, :, lanes(g)], grad_tokens.at[:, :, lanes(g)], store_sem.at[1, g]).start()
-
-    close_part(GROUPS - 1)
-    ends_recv[lat] = ends_send[...]
 
     def send_ends(p):
         pltpu.make_async_remote_copy(
@@ -503,7 +499,20 @@
             device_id_type=MESH,
         ).start()
 
-    each_peer(send_ends)
+    @pl.loop(0, GROUPS)
+    def _(g):
+        wait_field(grad, recv_sem, GRAD, g)
+        sum_part(g)
+        for k in range(GROUPS):
+            pl.when(g == k)(functools.partial(close_part, k))
+
+        @pl.when(g == GROUPS - 1)
+        def _():
+            ends_recv[lat] = ends_send[...]
+            each_peer(send_ends)
+
+        finish_tokens(g)
+
     wait_bytes(ends_recv, small_recv.at[2])
     ends_out[...] = jnp.sum(ends_recv[...], axis=0)
     wait_bytes(params_out, small_recv.at[1])
@@ -599,7 +608,6 @@
     lonh, lonl = pair(lon2, lon)
     lonih, lonil = pair(lon.T, lon2.T)
     hbm, vmem = pl.BlockSpec(memory_space=pl.ANY), pl.BlockSpec(memory_space=pltpu.VMEM)
-    smem = pl.BlockSpec(memory_space=pltpu.SMEM)
     field = jax.ShapeDtypeStruct((32, 2, CH * LON), bf16)
     V, D = pltpu.VMEM, pltpu.SemaphoreType.DMA
     fld = V((32, 2, CH * LON), bf16)
@@ -611,7 +619,7 @@
     ]
     return pl.pallas_call(
         mega_kernel,
-        in_specs=[smem, smem] + [hbm] * (len(ins) - 2),
+        in_specs=[hbm] * len(ins),
         out_specs=[hbm, hbm, vmem, vmem],
         out_shape=[
             field, field,
@@ -619,7 +627,7 @@
             jax.ShapeDtypeStruct((2, 128), f32),
         ],
         scratch_shapes=[
-            *[V(x.shape, x.dtype) for x in ins[4:]], D((len(ins) - 4,)),
+            *[V(x.shape, x.dtype) for x in ins[4:]], pltpu.SMEM((CH,), f32), pltpu.SMEM((CH,), f32), D((len(ins) - 2,)),
             V((GROUPS, 1, SPAN), f32), V((GROUPS, 1, SPAN), f32), V((192, 192), f32), V((8, 256), f32), V((256, 8), f32),
             fld, fld, V((2, 32, 2, CH * LON), bf16), fld, fld, fld, fld,
             V((2, 2, LAT_ROWS, CH, 128), f32),

time: 232 us -> 230 us (level)
  no operation moved by 1% of the time
where the time goes in v5:
time: 230 us
  Pallas kernels  230 us (100%)
    pallas_call x1, Pallas kernels, mega(): pl.pallas_call(mega_kernel, in_specs=[hbm] * len(ins), out_specs=[hbm, hb...  225 us
    pallas_call x1, Pallas kernels, finish(): pl.pallas_call(finish_kernel, in_specs=[hbm] * 4, out_specs=[hbm] * 8, ou...  4.81 us

profile of v5, /device:TPU:1, one launch (start us, length us, event | category | flops | bytes accessed | tf_op | source)
XLA Modules:
  0.0 230.4 jit_solution(4104842172750383904)
XLA Ops:
  0.6 224.8 %afno.1 = (bf16[32,2,17280]{2,1,0:T(2,128)(2,1)}, bf16[32,2,17280]{2,1,0:T(2,128)(2,1)}, bf16[32,16,128]{2,1,0:T(8,128)(2,1)}, f32[2,128]{1,0:T(2,128)}) custom-call(f32[96]{0:T(128)} %gain_hbm.1, f32[96]{0:T(128)} %shift_hbm.1, bf16[32,2,17280]{2,1,0:T(2,128)(2,1)} %tokens.1, bf16[32,2,17280]{2,1,0:T(2,128)(2,1)} %upstream.1, f32[2,1,96,96]{3,2,1,0:T(8,128)} %w1_hbm.1, ...), custom_call_target="tpu_custom_call" | custom-call | tf_op jit(solution)/shard_map/afno/pallas_call | solution.py:620
  225.4 4.8 %finish.1 = (bf16[32,2,17280]{2,1,0:T(2,128)(2,1)}, bf16[32,2,17280]{2,1,0:T(2,128)(2,1)}, f32[2,1,96,96]{3,2,1,0:T(8,128)}, f32[2,1,96]{2,1,0:T(1,128)}, f32[2,...) custom-call(bf16[32,2,17280]{2,1,0:T(2,128)(2,1)} %get-tuple-element.20.result, ...), custom_call_target="tpu_custom_call" | custom-call | tf_op jit(solution)/shard_map/finish/pallas_call | solution.py:587
